TPU v7x, 32 devices: a whole 2x2x4 slice. The times are simulated.
32 devices in a mesh: blk: 16 (over z, y, x), row: 2 (over core).
Axes of the slice: x: 2, y: 2, z: 4, core: 2. Of those that a mesh axis runs over, the one named last changes fastest.
Arguments:
- genotypes: bfloat16 [128, 16, 2048], P('blk', None, 'row'), may hold values from 0 to 2
- assignment: int32 [16], replicated, may hold values from 0 to 15, each once
- snp_counts: int32 [16], replicated, may hold values from 1024 to 2048, as said below
- basis: float32 [16, 64, 2048], P('blk', None, 'row'), may hold values from -6 to 6
Outputs:
- image: float32 [16, 64, 2048], P('blk', None, 'row')
- new_basis: float32 [16, 64, 2048], P('blk', None, 'row')
- factor: float32 [16, 64, 64], P('blk')
Inputs may be any that keep to these rules, and one draw needn't show every extreme that they name: `assignment`: each block number appears exactly once. `snp_counts`: A block's SNPs fill its leading slots.
All inputs are finite; a program needn't handle non-finite values.
Results may differ from a plain program's by a relative error of at most 0.0021.
Values may be sent and summed in bfloat16 or wider, within the bound.
No kernel may reach another device: no remote copies, remote signals or barrier semaphores. Data moves between devices by JAX's collectives and lax.ppermute only.
A program may use at most 64 MiB of HBM per device.

v0:
```python
import jax
import jax.numpy as jnp
from jax import lax
from jax.sharding import PartitionSpec as P

epsilon = 1e-05
shrink_weight = 0.5


def body(genotypes, assignment, snp_counts, basis):
    ordered = jnp.take(genotypes, assignment, axis=1)
    regrouped = lax.all_to_all(ordered, "blk", split_axis=1, concat_axis=0, tiled=True)
    samples = regrouped.shape[0]
    owned = regrouped.shape[1]
    half_width = regrouped.shape[2]
    block_ids = lax.dynamic_slice_in_dim(assignment, lax.axis_index("blk") * owned, owned)
    catalog = jnp.arange(snp_counts.shape[0], dtype=jnp.int32)
    live_count = jnp.sum(
        jnp.where(block_ids[:, None] == catalog[None, :], snp_counts[None, :], 0), axis=1
    )
    columns = lax.axis_index("row") * half_width + jnp.arange(half_width, dtype=jnp.int32)
    live_mask = columns[None, :] < live_count[:, None]
    values = regrouped.astype(jnp.float32)
    col_mean = jnp.mean(values, axis=0)
    centered = values - col_mean[None]
    col_var = jnp.mean(centered * centered, axis=0)
    standard = jnp.where(
        live_mask[None], centered * lax.rsqrt(col_var + epsilon)[None], 0.0
    ).astype(jnp.bfloat16)
    inverse = 1.0 / samples
    partial_proj = jnp.einsum(
        "nbi,bri->brn",
        standard,
        basis,
        precision=lax.Precision.HIGHEST,
        preferred_element_type=jnp.float32,
    )
    projected = lax.psum(partial_proj, "row")
    product = (
        jnp.einsum(
            "nbi,brn->bri",
            standard,
            projected,
            precision=lax.Precision.HIGHEST,
            preferred_element_type=jnp.float32,
        )
        * inverse
    )
    image = shrink_weight * product + (1.0 - shrink_weight) * jnp.where(
        live_mask[:, None, :], basis, 0.0
    )
    gram_part = jnp.einsum("bri,bsi->brs", image, image, precision=lax.Precision.HIGHEST)
    gram_sum = lax.psum(gram_part, "row")
    factor = jnp.linalg.cholesky(gram_sum)
    new_basis = jax.scipy.linalg.solve_triangular(factor, image, lower=True)
    return (image, new_basis, factor)


def solution(mesh):
    in_specs = (P("blk", None, "row"), P(), P(), P("blk", None, "row"))
    out_specs = (P("blk", None, "row"), P("blk", None, "row"), P("blk", None, None))
    return jax.shard_map(body, mesh=mesh, in_specs=in_specs, out_specs=out_specs, check_vma=False)
```

profile of v0, /device:TPU:0, one launch (start us, length us, event | category | flops | bytes accessed | tf_op | source)
XLA Modules:
  0.0 44.3 jit_solution(11214147400684434349)
XLA Ops:
  0.6 0.0 copy-start
  0.6 0.0 copy-start.3
  0.7 0.7 %compare_and_fusion = pred[16]{0:T(512)(128)(4,1)S(1)} fusion(s32[16]{0:T(128)} %param.5), kind=kLoop, calls=%fused_computation.36 | loop fusion | flops 96 | bytes 80 | tf_op jit(solution)/shard_map/jit(_take)/and | solution.py:11
  1.4 0.0 copy-done.3
  1.4 0.2 copy-done
  1.6 1.3 %gather_fusion = bf16[16,8,1024]{2,0,1:T(8,128)(2,1)S(1)} fusion(bf16[8,16,1024]{2,1,0:T(8,128)(2,1)S(1)} %copy-done, s32[1024]{0:T(1024)S(1)} %pad_clamp_fusion), kind=kCustom, calls=%fused_computation | custom fusion | bytes 524352 | tf_op jit(solution)/shard_map/jit(_take)/gather | solution.py:11
  2.9 0.1 select_bitcast_fusion
  3.0 0.9 %copy.13 = bf16[8,16,1024]{2,0,1:T(8,128)(2,1)} copy(bf16[8,16,1024]{2,1,0:T(8,128)(2,1)S(1)} %select_bitcast_fusion) | data formatting | bytes 524288 | tf_op jit(solution)/shard_map/jit(_take)/select_n | solution.py:11
  3.9 8.3 %all-to-all-start = ((bf16[8,16,1024]{2,0,1:T(8,128)(2,1)}), bf16[8,16,1024]{2,0,1:T(8,128)(2,1)S(1)}, u32[]{:S(2)}, u32[]{:S(2)}) async-start(bf16[8,16,1024]{2,0,1:T(8,128)(2,1)} %copy.13), calls=%async_computation | async-start | bytes 524288 | tf_op jit(solution)/shard_map/all_to_all | solution.py:12
  12.2 0.6 %dynamic_slice.3 = s32[1]{0:T(128)} dynamic-slice(s32[16]{0:T(128)S(1)} %copy-done.3, s32[]{:T(128)S(6)} %select_n.50), dynamic_slice_sizes={1} | dynamic-slice | bytes 12 | tf_op jit(solution)/shard_map/dynamic_slice | solution.py:16
  12.8 0.0 copy-start.4
  12.8 0.7 %copy-done.4 = s32[16]{0:T(128)S(1)} copy-done((s32[16]{0:T(128)S(1)}, s32[16]{0:T(128)}, u32[]{:S(2)}) %copy-start.4) | copy-done | bytes 88
  13.5 1.3 %fusion.18 = s32[]{:T(128)} fusion(s32[16]{0:T(128)S(1)} %copy-done.4, s32[]{:T(128)} %bitcast), kind=kLoop, calls=%fused_computation.38 | loop fusion | flops 47 | bytes 72 | tf_op jit(solution)/shard_map/reduce_sum | solution.py:18
  14.8 0.7 %add_compare_fusion = pred[1024]{0:T(1024)(128)(4,1)S(1)} fusion(s32[]{:T(128)} %fusion.18, s32[]{:T(128)S(6)} %mul.56), kind=kLoop, calls=%fused_computation.32 | loop fusion | flops 2048 | bytes 1032 | tf_op jit(solution)/shard_map/lt | solution.py:22
  15.4 0.0 copy-start.2
  15.4 6.7 %all-to-all-done = bf16[8,16,1024]{2,0,1:T(8,128)(2,1)S(1)} async-done(((bf16[8,16,1024]{2,0,1:T(8,128)(2,1)}), bf16[8,16,1024]{2,0,1:T(8,128)(2,1)S(1)}, u32[]{:S(2)}, u32[]{:S(2)}) %all-to-all-start) | async-done | bytes 262176 | tf_op jit(solution)/shard_map/all_to_all | solution.py:12
  22.1 0.1 convert_reduce_fusion
  22.2 0.1 fusion.4
  22.3 0.0 copy-done.2
  22.3 0.4 convolution_bitcast_fusion.2
  22.7 3.4 %psum.14 = f32[64,128]{1,0:T(8,128)S(1)} all-reduce(f32[64,128]{1,0:T(8,128)S(1)} %convolution_bitcast_fusion.2), channel_id=1, replica_groups=mesh['blk'=16,'row'=2] {'row'}, use_global_device_ids=true, to_apply=%region_3.4 | all-reduce | flops 8192 | bytes 65536 | tf_op jit(solution)/shard_map/psum | solution.py:38
  26.1 0.3 fusion.1
  26.4 0.0 copy-start.1
  26.4 0.4 convolution_bitcast_fusion.1
  26.8 3.6 %psum.15 = f32[1,64,64]{1,2,0:T(8,128)S(1)} all-reduce(f32[1,64,64]{1,2,0:T(8,128)S(1)} %convolution_bitcast_fusion.1), channel_id=1, replica_groups=mesh['blk'=16,'row'=2] {'row'}, use_global_device_ids=true, to_apply=%region_4.5 | all-reduce | flops 4096 | bytes 32768 | tf_op jit(solution)/shard_map/psum | solution.py:53
  30.3 0.1 copy.15
  30.4 5.8 %custom-call.8 = f32[1,64,64]{2,1,0:T(8,128)S(1)} custom-call(f32[1,64,64]{2,1,0:T(8,128)S(1)} %fusion.16), custom_call_target="Cholesky" | custom-call | tf_op jit(solution)/shard_map/jit(cholesky)/cholesky | solution.py:54
  36.3 0.6 %compare_reduce_fusion = pred[]{:T(512)} fusion(f32[64]{0:T(128)S(1)} %select_reduce_fusion), kind=kLoop, calls=%fused_computation.35 | loop fusion | flops 127 | bytes 257 | tf_op jit(solution)/shard_map/jit(cholesky)/cholesky | solution.py:54
  37.0 1.3 %fusion.17 = (f32[1,64,64]{2,1,0:T(8,128)S(1)}, f32[1,64,64]{2,1,0:T(8,128)}) fusion(f32[1,64,64]{2,1,0:T(8,128)S(1)} %custom-call.8, pred[]{:T(512)} %compare_reduce_fusion), kind=kLoop, calls=%fused_computation.29 | loop fusion | flops 16384 | bytes 49153 | tf_op jit(solution)/shard_map/jit(_solve_triangular)/triangular_solve | solution.py:55
  38.2 4.9 %custom-call.9 = f32[1,64,64]{1,2,0:T(8,128)S(1)} custom-call(f32[1,64,64]{2,1,0:T(8,128)S(1)} %get-tuple-element.3), custom_call_target="InvertDiagBlocksLowerTriangular" | custom-call | tf_op jit(solution)/shard_map/jit(_solve_triangular)/triangular_solve | solution.py:55
  43.1 0.0 copy-done.1
  43.1 1.1 %convolution_bitcast_fusion = f32[1,64,1024]{2,1,0:T(8,128)} fusion(f32[1,64,1024]{2,1,0:T(8,128)S(1)} %fusion.1, f32[1,64,64]{1,2,0:T(8,128)S(1)} %custom-call.9), kind=kOutput, calls=%fused_computation.3 | convolution fusion | flops 50331648 | bytes 540672 | tf_op jit(solution)/shard_map/jit(_solve_triangular)/triangular_solve | solution.py:55
  (6 shorter events, 0.1 us)
Async XLA Ops:
  0.6 1.0 %copy-start = (bf16[8,16,1024]{2,1,0:T(8,128)(2,1)S(1)}, bf16[8,16,1024]{2,1,0:T(8,128)(2,1)}, u32[]{:S(2)}) copy-start(bf16[8,16,1024]{2,1,0:T(8,128)(2,1)} %param.4) | copy-start | bytes 786436
  0.6 0.7 %copy-start.3 = (s32[16]{0:T(128)S(1)}, s32[16]{0:T(128)}, u32[]{:S(2)}) copy-start(s32[16]{0:T(128)} %param.5) | copy-start | bytes 196
  3.9 18.2 %all-to-all-start = ((bf16[8,16,1024]{2,0,1:T(8,128)(2,1)}), bf16[8,16,1024]{2,0,1:T(8,128)(2,1)S(1)}, u32[]{:S(2)}, u32[]{:S(2)}) async-start(bf16[8,16,1024]{2,0,1:T(8,128)(2,1)} %copy.13), calls=%async_computation | async-start | bytes 524288 | tf_op jit(solution)/shard_map/all_to_all | solution.py:12
  12.8 0.7 %copy-start.4 = (s32[16]{0:T(128)S(1)}, s32[16]{0:T(128)}, u32[]{:S(2)}) copy-start(s32[16]{0:T(128)} %param.6) | copy-start | bytes 196
  15.4 6.9 %copy-start.2 = (f32[1,64,1024]{2,1,0:T(8,128)S(1)}, f32[1,64,1024]{2,1,0:T(8,128)}, u32[]{:S(2)}) copy-start(f32[1,64,1024]{2,1,0:T(8,128)} %param.7) | copy-start | bytes 786436
  26.4 16.8 %copy-start.1 = (f32[1,64,1024]{2,1,0:T(8,128)}, f32[1,64,1024]{2,1,0:T(8,128)S(1)}, u32[]{:S(2)}) copy-start(f32[1,64,1024]{2,1,0:T(8,128)S(1)} %fusion.1) | copy-start | bytes 786436
where the time goes:
time: 44.6 us; the launch traced here: 44.3 us
  other arithmetic  15.6 us (35%)
  starting transfers between devices  8.34 us (19%)
  blocking collectives  6.97 us (16%)
  waiting for transfers between devices  6.68 us (15%)
  local copies, waits for them, and re-layouts  3.73 us (8%)
  matrix products  2.15 us (5%)
  between operations  0.79 us (2%)
    all_to_all x1, starting transfers between devices, body(): lax.all_to_all(ordered, 'blk', split_axis=1, concat_axis=0, tiled=True)  8.34 us
    all_to_all x1, waiting for transfers between devices, body(): lax.all_to_all(ordered, 'blk', split_axis=1, concat_axis=0, tiled=True)  6.68 us
    another operation x3, other arithmetic, body(): factor = jnp.linalg.cholesky(gram_sum)  6.52 us
    another operation x2, other arithmetic, body(): new_basis = jax.scipy.linalg.solve_triangular(factor, image, lower=True)  6.16 us
    psum x1, blocking collectives, body(): gram_sum = lax.psum(gram_part, 'row')  3.57 us
    psum x1, blocking collectives, body(): projected = lax.psum(partial_proj, 'row')  3.41 us
    gather x1, local copies, waits for them, and re-layouts, body(): ordered = jnp.take(genotypes, assignment, axis=1)  1.31 us
    reduce_sum x1, other arithmetic, body(): jnp.sum(jnp.where(block_ids[:, None] == catalog[None, :], snp_counts[None...  1.27 us
  transfers between devices with their start and end apart: 1, of which 1 were waited for; matrix products, arithmetic and copies ran while one was open for 6% of the time, Pallas kernels for 0%

commit v1 on v0

v1 whole, which is shorter than its diff:
```python
import functools

import jax
import jax.numpy as jnp
from jax import lax
from jax.experimental import pallas as pl
from jax.experimental.pallas import tpu as pltpu
from jax.sharding import PartitionSpec as P

epsilon = 1e-05
shrink_weight = 0.5

VMEM = pltpu.VMEM
SMEM = pltpu.SMEM
HIGHEST = lax.Precision.HIGHEST
f32 = jnp.float32
bf16 = jnp.bfloat16


def dot(x, y, dims, precision=None):
    return lax.dot_general(x, y, (dims, ((), ())), precision=precision, preferred_element_type=f32)


NN = ((1,), (0,))
NT = ((1,), (1,))


def in_vmem(n):
    return [pl.BlockSpec(memory_space=VMEM)] * n


def split3(x):
    high = x.astype(bf16)
    rest = x - high.astype(f32)
    mid = rest.astype(bf16)
    low = (rest - mid.astype(f32)).astype(bf16)
    return high, mid, low


def order_kernel(samples, blocks, group, assignment, rows_ref, out_ref):
    shape = (samples, samples * blocks)
    column = lax.broadcasted_iota(jnp.int32, shape, 1)
    start = lax.broadcasted_iota(jnp.int32, shape, 0) * blocks
    for first in range(0, blocks, group):
        picks = [
            jnp.where(column == start + assignment[first + s], 1.0, 0.0).astype(f32)
            for s in range(group)
        ]
        pick = jnp.concatenate(picks, axis=0).astype(bf16)
        out_ref[first * samples : (first + group) * samples, :] = dot(
            pick, rows_ref[...], NN
        ).astype(bf16)


def basis_kernel(half, assignment, snp_counts, basis_ref, split_ref, masked_ref, live_ref, gram_ref):
    count = snp_counts[assignment[lax.axis_index("blk")]]
    basis = basis_ref[...]
    rank = basis.shape[0]
    column = lax.broadcasted_iota(jnp.int32, (8, half), 1) + lax.axis_index("row") * half
    live = jnp.where(column < count, 1.0, 0.0).astype(f32)
    live_ref[...] = live
    masked = basis * live[:1]
    masked_ref[...] = masked * (1.0 - shrink_weight)
    for i, piece in enumerate(split3(basis)):
        split_ref[i * rank : (i + 1) * rank, :] = piece
    gram_ref[...] = dot(masked, masked, NT, HIGHEST)


def project_kernel(rank, values_ref, live_ref, split_ref, standard_ref, part_ref):
    values = values_ref[...].astype(f32)
    samples = values.shape[0]
    mean = jnp.sum(values, axis=0, keepdims=True) * (1.0 / samples)
    centered = values - mean
    var = jnp.sum(centered * centered, axis=0, keepdims=True) * (1.0 / samples)
    scale = lax.rsqrt(var + epsilon)
    standard = jnp.where(live_ref[:1] > 0.0, centered * scale, 0.0).astype(bf16)
    standard_ref[...] = standard
    wide = dot(split_ref[...], standard, NT)
    part_ref[:rank, :] = wide[:rank] + (wide[rank : 2 * rank] + wide[2 * rank :])
    part_ref[rank:, :] = dot(standard, standard, NT)


def factor_and_inverse(gram, panel):
    rank = gram.shape[0]
    eye = jnp.where(
        lax.broadcasted_iota(jnp.int32, (rank, rank), 0)
        == lax.broadcasted_iota(jnp.int32, (rank, rank), 1),
        1.0,
        0.0,
    ).astype(f32)
    full = jnp.concatenate([gram, eye], axis=1)
    lanes = 2 * rank
    tiles = rank // 8
    work = [full[8 * t : 8 * t + 8] for t in range(tiles)]
    sublane = lax.broadcasted_iota(jnp.int32, (8, lanes), 0)
    lane = lax.broadcasted_iota(jnp.int32, (8, lanes), 1)
    lower = [jnp.zeros((8, lanes), f32) for _ in range(tiles)]

    def row(tile, r):
        return jnp.broadcast_to(tile[r : r + 1, :], (8, lanes))

    for first in range(0, rank, panel):
        base = first // 8
        cols = [
            [
                jnp.broadcast_to(work[t][:, first + j : first + j + 1], (8, lanes))
                for t in range(base, tiles)
            ]
            for j in range(panel)
        ]
        for j in range(panel):
            k = first + j
            t0, r = k // 8, k % 8
            col = cols[j]
            root = lax.rsqrt(row(col[t0 - base], r))
            low = [c * root for c in col[t0 - base :]]
            low[0] = jnp.where(sublane >= r, low[0], 0.0)
            mult = [c * root for c in low]
            mult[0] = jnp.where(sublane > r, mult[0], 0.0)
            for j2 in range(j + 1, panel):
                other = cols[j2]
                pivot = row(other[t0 - base], r)
                for t in range(t0, tiles):
                    other[t - base] = other[t - base] - mult[t - t0] * pivot
            pivot = row(work[t0], r)
            for t in range(t0, tiles):
                work[t] = work[t] - mult[t - t0] * pivot
                lower[t] = jnp.where(lane == k, low[t - t0], lower[t])
            work[t0] = jnp.where(sublane == r, pivot * root, work[t0])
    lower = jnp.concatenate(lower, axis=0)[:, :rank]
    inverse = jnp.concatenate(work, axis=0)[:, rank:]
    return lower, inverse


def finish_kernel(
    scale, own_ref, peer_ref, own_gram_ref, peer_gram_ref, standard_ref, masked_ref,
    image_ref, new_ref, factor_ref, image_buf, new_buf, sems,
):
    rank = masked_ref.shape[0]
    total = own_ref[...] + peer_ref[...]
    proj = total[:rank]
    cross = total[rank:]
    samples = cross.shape[0]
    keep = 1.0 - shrink_weight
    diagonal = lax.broadcasted_iota(jnp.int32, (samples, samples), 0) == lax.broadcasted_iota(
        jnp.int32, (samples, samples), 1
    )
    middle = cross * (scale * scale) + jnp.where(diagonal, 2.0 * scale * keep, 0.0).astype(f32)
    gram = dot(dot(proj, middle, NN, HIGHEST), proj, NT, HIGHEST)
    gram = gram + (own_gram_ref[...] + peer_gram_ref[...]) * (keep * keep)
    rows = jnp.concatenate(split3(proj * scale), axis=0)
    wide = dot(rows, standard_ref[...], NN)
    image = wide[:rank] + (wide[rank : 2 * rank] + wide[2 * rank :]) + masked_ref[...]
    image_buf[...] = image
    image_copy = pltpu.make_async_copy(image_buf, image_ref, sems.at[0])
    image_copy.start()
    lower, inverse = factor_and_inverse(gram, 8)
    factor_ref[...] = lower
    new_buf[...] = dot(inverse, image, NN, HIGHEST)
    new_copy = pltpu.make_async_copy(new_buf, new_ref, sems.at[1])
    new_copy.start()
    image_copy.wait()
    new_copy.wait()


def body(genotypes, assignment, snp_counts, basis):
    samples, blocks, half = genotypes.shape
    owned, rank, _ = basis.shape
    assert owned == 1
    group = 16 if blocks % 16 == 0 else blocks
    scalars = [pl.BlockSpec(memory_space=SMEM)]
    ordered = pl.pallas_call(
        functools.partial(order_kernel, samples, blocks, group),
        out_shape=jax.ShapeDtypeStruct((blocks * samples, half), bf16),
        in_specs=scalars + in_vmem(1),
        out_specs=pl.BlockSpec(memory_space=VMEM),
        name="order",
    )(assignment, genotypes.reshape(samples * blocks, half))
    regrouped = lax.all_to_all(
        ordered.reshape(blocks, samples, half), "blk", split_axis=0, concat_axis=0, tiled=True
    )
    split, masked, live, basis_gram = pl.pallas_call(
        functools.partial(basis_kernel, half),
        out_shape=[
            jax.ShapeDtypeStruct((3 * rank, half), bf16),
            jax.ShapeDtypeStruct((rank, half), f32),
            jax.ShapeDtypeStruct((8, half), f32),
            jax.ShapeDtypeStruct((rank, rank), f32),
        ],
        in_specs=scalars * 2 + in_vmem(1),
        out_specs=in_vmem(4),
        cost_estimate=pl.CostEstimate(flops=2**26, bytes_accessed=2**20, transcendentals=0),
        name="basis",
    )(assignment, snp_counts, basis[0])
    swap = [(0, 1), (1, 0)]
    peer_basis_gram = lax.ppermute(basis_gram, "row", swap)
    total = blocks * samples
    standard, part = pl.pallas_call(
        functools.partial(project_kernel, rank),
        out_shape=[
            jax.ShapeDtypeStruct((total, half), bf16),
            jax.ShapeDtypeStruct((rank + total, total), f32),
        ],
        in_specs=in_vmem(3),
        out_specs=in_vmem(2),
        name="project",
    )(regrouped.reshape(total, half), live, split)
    peer_part = lax.ppermute(part, "row", swap)
    image, new_basis, factor = pl.pallas_call(
        functools.partial(finish_kernel, shrink_weight / total),
        out_shape=[
            jax.ShapeDtypeStruct((rank, half), f32),
            jax.ShapeDtypeStruct((rank, half), f32),
            jax.ShapeDtypeStruct((rank, rank), f32),
        ],
        in_specs=in_vmem(6),
        out_specs=[pl.BlockSpec(memory_space=pl.ANY)] * 2 + in_vmem(1),
        scratch_shapes=[
            pltpu.VMEM((rank, half), f32),
            pltpu.VMEM((rank, half), f32),
            pltpu.SemaphoreType.DMA((2,)),
        ],
        name="finish",
    )(part, peer_part, basis_gram, peer_basis_gram, standard, masked)
    return image[None], new_basis[None], factor[None]


def solution(mesh):
    in_specs = (P("blk", None, "row"), P(), P(), P("blk", None, "row"))
    out_specs = (P("blk", None, "row"), P("blk", None, "row"), P("blk", None, None))
    return jax.shard_map(body, mesh=mesh, in_specs=in_specs, out_specs=out_specs, check_vma=False)
```

time: 44.6 us -> 31.3 us (0.70)
  other arithmetic: 15.6 us -> 0 us
  Pallas kernels: 0 us -> 11.2 us
  blocking collectives: 6.97 us -> 0 us
  local copies, waits for them, and re-layouts: 3.73 us -> 1.35 us
  waiting for transfers between devices: 6.68 us -> 8.95 us
  matrix products: 2.15 us -> 0 us
  starting transfers between devices: 8.34 us -> 8.85 us
    another operation x5 -> x0, other arithmetic: 12.7 us -> none  [the longest x3 6.52 us: body(): factor = jnp.linalg.cholesky(gram_sum)]
    pallas_call x0 -> x4, Pallas kernels: none -> 11.2 us  [the longest x1 5.21 us: body(): pl.pallas_call(functools.partial(finish_kernel, shrink_weight / total), o...]
    psum x2 -> x0, blocking collectives: 6.97 us -> none  [the longest x1 3.57 us: body(): gram_sum = lax.psum(gram_part, 'row')]
    reduce_sum x3 -> x0, other arithmetic: 1.41 us -> none  [the longest x1 1.27 us: body(): jnp.sum(jnp.where(block_ids[:, None] == catalog[None, :], snp_counts[None...]
    gather x1 -> x0, local copies, waits for them, and re-layouts: 1.31 us -> none  [body(): ordered = jnp.take(genotypes, assignment, axis=1)]
    all_to_all x1, waiting for transfers between devices: 6.68 us -> 7.9 us  [body(): lax.all_to_all(ordered.reshape(blocks, samples, half), 'blk', split_axis=...]
    another operation x1 -> x0, matrix products: 1.12 us -> none  [body(): new_basis = jax.scipy.linalg.solve_triangular(factor, image, lower=True)]
    ppermute x0 -> x2, waiting for transfers between devices: none -> 1.05 us  [the longest x1 1.05 us: body(): peer_basis_gram = lax.ppermute(basis_gram, 'row', swap)]
  transfers between devices with their start and end apart: 1 -> 3, of which waited for: 1 -> 2; matrix products, arithmetic and copies ran while one was open for 6% -> 0% of each run, Pallas kernels for 0% -> 6%
where the time goes in v1:
time: 31.3 us; the launch traced here: 31 us
  Pallas kernels  11.2 us (36%)
  waiting for transfers between devices  8.95 us (29%)
  starting transfers between devices  8.85 us (28%)
  local copies, waits for them, and re-layouts  1.35 us (4%)
  between operations  0.65 us (2%)
    all_to_all x1, starting transfers between devices, body(): lax.all_to_all(ordered.reshape(blocks, samples, half), 'blk', split_axis=...  8.34 us
    all_to_all x1, waiting for transfers between devices, body(): lax.all_to_all(ordered.reshape(blocks, samples, half), 'blk', split_axis=...  7.9 us
    pallas_call x1, Pallas kernels, body(): pl.pallas_call(functools.partial(finish_kernel, shrink_weight / total), o...  5.21 us
    pallas_call x1, Pallas kernels, body(): pl.pallas_call(functools.partial(project_kernel, rank), out_shape=[jax.Sh...  2.18 us
    pallas_call x1, Pallas kernels, body(): pl.pallas_call(functools.partial(basis_kernel, half), out_shape=[jax.Shap...  1.97 us
    pallas_call x1, Pallas kernels, body(): pl.pallas_call(functools.partial(order_kernel, samples, blocks, group), o...  1.88 us
    unnamed x8, local copies, waits for them, and re-layouts  1.35 us
    ppermute x1, waiting for transfers between devices, body(): peer_basis_gram = lax.ppermute(basis_gram, 'row', swap)  1.05 us
  transfers between devices with their start and end apart: 3, of which 2 were waited for; matrix products, arithmetic and copies ran while one was open for 0% of the time, Pallas kernels for 6%

profile of v1, /device:TPU:0, one launch (start us, length us, event | category | flops | bytes accessed | tf_op | source)
XLA Modules:
  0.0 31.0 jit_solution(4808498487941888792)
XLA Ops:
  0.6 1.9 %order.1 = bf16[128,1024]{1,0:T(8,128)(2,1)} custom-call(s32[16]{0:T(128)} %assignment.3, bf16[128,1024]{1,0:T(8,128)(2,1)} %bitcast.9), custom_call_target="tpu_custom_call" | custom-call | tf_op jit(solution)/shard_map/order/pallas_call | solution.py:172
  2.5 8.3 %all-to-all-start = ((bf16[16,8,1024]{2,1,0:T(8,128)(2,1)}), bf16[16,8,1024]{2,1,0:T(8,128)(2,1)S(1)}, u32[]{:S(2)}, u32[]{:S(2)}) async-start(bf16[16,8,1024]{2,1,0:T(8,128)(2,1)} %bitcast.7), calls=%async_computation | async-start | bytes 524288 | tf_op jit(solution)/shard_map/all_to_all | solution.py:179
  10.9 2.0 %basis.1 = (bf16[192,1024]{1,0:T(8,128)(2,1)}, f32[64,1024]{1,0:T(8,128)}, f32[8,1024]{1,0:T(8,128)}, f32[64,64]{1,0:T(8,128)}) custom-call(s32[16]{0:T(128)} %assignment.3, s32[16]{0:T(128)} %snp_counts.1, f32[64,1024]{1,0:T(8,128)} %bitcast.10), custom_call_target="tpu_custom_call" | custom-call | flops 67108864 | bytes 1048576 | tf_op jit(solution)/shard_map/basis/pallas_call | solution.py:182
  12.8 7.9 %all-to-all-done = bf16[16,8,1024]{2,1,0:T(8,128)(2,1)S(1)} async-done(((bf16[16,8,1024]{2,1,0:T(8,128)(2,1)}), bf16[16,8,1024]{2,1,0:T(8,128)(2,1)S(1)}, u32[]{:S(2)}, u32[]{:S(2)}) %all-to-all-start) | async-done | bytes 262176 | tf_op jit(solution)/shard_map/all_to_all | solution.py:179
  20.7 0.0 copy-start
  20.7 0.7 %copy-done = bf16[16,8,1024]{2,1,0:T(8,128)(2,1)} copy-done((bf16[16,8,1024]{2,1,0:T(8,128)(2,1)}, bf16[16,8,1024]{2,1,0:T(8,128)(2,1)S(1)}, u32[]{:S(2)}) %copy-start) | copy-done | bytes 262168
  21.4 0.0 copy-start.2
  21.4 2.2 %project.1 = (bf16[128,1024]{1,0:T(8,128)(2,1)}, f32[192,128]{1,0:T(8,128)}) custom-call(bf16[128,1024]{1,0:T(8,128)(2,1)} %bitcast.8, f32[8,1024]{1,0:T(8,128)} %get-tuple-element.12.live_ref, bf16[192,1024]{1,0:T(8,128)(2,1)} %get-tuple-element.13.split_ref), custom_call_target="tpu_custom_call" | custom-call | tf_op jit(solution)/shard_map/project/pallas_call | solution.py:198
  23.6 0.0 collective-permute-start
  23.6 0.0 copy-done.2
  23.6 0.5 %collective-permute-start.1 = (f32[64,64]{1,0:T(8,128)S(1)}, f32[64,64]{1,0:T(8,128)S(1)}, u32[]{:S(2)}, u32[]{:S(2)}) collective-permute-start(f32[64,64]{1,0:T(8,128)S(1)} %copy-done.2), channel_id=1, source_target_pairs={{0,1},{1,0},{2,3},{3,2},{4,5},{5,4},{6,7},{7,6},{8,9},{9,8},{10,11... | collective-permute-start | bytes 49160 | tf_op jit(solution)/shard_map/ppermute | solution.py:196
  24.1 1.0 %collective-permute-done.1.peer_gram_ref = f32[64,64]{1,0:T(8,128)S(1)} collective-permute-done((f32[64,64]{1,0:T(8,128)S(1)}, f32[64,64]{1,0:T(8,128)S(1)}, u32[]{:S(2)}, u32[]{:S(2)}) %collective-permute-start.1) | collective-permute-done | bytes 16416 | tf_op jit(solution)/shard_map/ppermute | solution.py:196
  25.2 0.0 copy-start.3
  25.2 0.0 collective-permute-done.peer_ref
  25.2 0.0 copy-start.1
  25.2 0.6 %copy-done.3 = f32[64,64]{1,0:T(8,128)} copy-done((f32[64,64]{1,0:T(8,128)}, f32[64,64]{1,0:T(8,128)S(1)}, u32[]{:S(2)}) %copy-start.3) | copy-done | bytes 16408
  25.8 0.0 copy-done.1
  25.8 5.2 %finish.1 = (f32[64,1024]{1,0:T(8,128)}, f32[64,1024]{1,0:T(8,128)}, f32[64,64]{1,0:T(8,128)}) custom-call(f32[192,128]{1,0:T(8,128)} %get-tuple-element.14.own_ref, f32[192,128]{1,0:T(8,128)} %copy-done.1, f32[64,64]{1,0:T(8,128)} %get-tuple-element.15.own_gram_ref, f32[64,64]{1,0:T(8,128)} %copy-done.3, bf16[128,1024]{1,0:T(8,128)(2,1)} %get-tuple-element.16.standard_ref, ...), custom_call_target="tpu_custom_call" | custom-call | tf_op jit(solution)/shard_map/finish/pallas_call | solution.py:209
Async XLA Ops:
  2.5 18.2 %all-to-all-start = ((bf16[16,8,1024]{2,1,0:T(8,128)(2,1)}), bf16[16,8,1024]{2,1,0:T(8,128)(2,1)S(1)}, u32[]{:S(2)}, u32[]{:S(2)}) async-start(bf16[16,8,1024]{2,1,0:T(8,128)(2,1)} %bitcast.7), calls=%async_computation | async-start | bytes 524288 | tf_op jit(solution)/shard_map/all_to_all | solution.py:179
  20.7 0.7 %copy-start = (bf16[16,8,1024]{2,1,0:T(8,128)(2,1)}, bf16[16,8,1024]{2,1,0:T(8,128)(2,1)S(1)}, u32[]{:S(2)}) copy-start(bf16[16,8,1024]{2,1,0:T(8,128)(2,1)S(1)} %all-to-all-done) | copy-start | bytes 786436
  21.4 2.2 %copy-start.2 = (f32[64,64]{1,0:T(8,128)S(1)}, f32[64,64]{1,0:T(8,128)}, u32[]{:S(2)}) copy-start(f32[64,64]{1,0:T(8,128)} %get-tuple-element.15.own_gram_ref) | copy-start | bytes 49156
  23.6 1.6 %collective-permute-start = (f32[192,128]{1,0:T(8,128)}, f32[192,128]{1,0:T(8,128)S(1)}, u32[]{:S(2)}, u32[]{:S(2)}) collective-permute-start(f32[192,128]{1,0:T(8,128)} %get-tuple-element.14.own_ref), channel_id=1, source_target_pairs={{0,1},{1,0},{2,3},{3,2},{4,5},{5,4},{6,7},{7,6},{8,9},{9,8},{10,11... | collective-permute-start | bytes 294920 | tf_op jit(solution)/shard_map/ppermute | solution.py:208
  23.6 1.6 %collective-permute-start.1 = (f32[64,64]{1,0:T(8,128)S(1)}, f32[64,64]{1,0:T(8,128)S(1)}, u32[]{:S(2)}, u32[]{:S(2)}) collective-permute-start(f32[64,64]{1,0:T(8,128)S(1)} %copy-done.2), channel_id=1, source_target_pairs={{0,1},{1,0},{2,3},{3,2},{4,5},{5,4},{6,7},{7,6},{8,9},{9,8},{10,11... | collective-permute-start | bytes 49160 | tf_op jit(solution)/shard_map/ppermute | solution.py:196
  25.2 0.6 %copy-start.3 = (f32[64,64]{1,0:T(8,128)}, f32[64,64]{1,0:T(8,128)S(1)}, u32[]{:S(2)}) copy-start(f32[64,64]{1,0:T(8,128)S(1)} %collective-permute-done.1.peer_gram_ref) | copy-start | bytes 49156
  25.2 0.6 %copy-start.1 = (f32[192,128]{1,0:T(8,128)}, f32[192,128]{1,0:T(8,128)S(1)}, u32[]{:S(2)}) copy-start(f32[192,128]{1,0:T(8,128)S(1)} %collective-permute-done.peer_ref) | copy-start | bytes 294916

commit v2 on v1

v2 whole, which is shorter than its diff:
```python
import functools

import jax
import jax.numpy as jnp
from jax import lax
from jax.experimental import pallas as pl
from jax.experimental.pallas import tpu as pltpu
from jax.sharding import PartitionSpec as P

epsilon = 1e-05
WIDTH = 256
PANELS = tuple((f, f, f + 8) for f in range(0, 64, 8))
shrink_weight = 0.5

VMEM = pltpu.VMEM
SMEM = pltpu.SMEM
HIGHEST = lax.Precision.HIGHEST
f32 = jnp.float32
bf16 = jnp.bfloat16


def dot(x, y, dims, precision=None):
    return lax.dot_general(x, y, (dims, ((), ())), precision=precision, preferred_element_type=f32)


NN = ((1,), (0,))
NT = ((1,), (1,))


def in_vmem(n):
    return [pl.BlockSpec(memory_space=VMEM)] * n


def split3(x):
    high = x.astype(bf16)
    rest = x - high.astype(f32)
    mid = rest.astype(bf16)
    low = (rest - mid.astype(f32)).astype(bf16)
    return high, mid, low


def order_kernel(
    samples, blocks, group, width, assignment_ref, rows_ref, out_ref,
    assignment, rows, ordered, scalar_sem, in_sems, out_sems,
):
    pieces = rows_ref.shape[1] // width
    fetch = pltpu.make_async_copy(assignment_ref, assignment, scalar_sem)
    fetch.start()
    loads, stores = [], []
    for i in range(pieces):
        columns = pl.ds(i * width, width)
        loads.append(
            pltpu.make_async_copy(rows_ref.at[:, columns], rows.at[:, columns], in_sems.at[i])
        )
        stores.append(
            pltpu.make_async_copy(ordered.at[:, columns], out_ref.at[:, columns], out_sems.at[i])
        )
        loads[i].start()
    shape = (samples, samples * blocks)
    column = lax.broadcasted_iota(jnp.int32, shape, 1)
    start = lax.broadcasted_iota(jnp.int32, shape, 0) * blocks
    fetch.wait()
    picks = []
    for first in range(0, blocks, group):
        ones = [
            jnp.where(column == start + assignment[first + s], 1.0, 0.0).astype(f32)
            for s in range(group)
        ]
        picks.append(jnp.concatenate(ones, axis=0).astype(bf16))
    for i in range(pieces):
        loads[i].wait()
        columns = slice(i * width, (i + 1) * width)
        for g, pick in enumerate(picks):
            span = slice(g * group * samples, (g + 1) * group * samples)
            ordered[span, columns] = dot(pick, rows[:, columns], NN).astype(bf16)
        stores[i].start()
    for store in stores:
        store.wait()


def basis_kernel(half, assignment, snp_counts, basis_ref, split_ref, masked_ref, live_ref, gram_ref):
    count = snp_counts[assignment[lax.axis_index("blk")]]
    basis = basis_ref[...]
    rank = basis.shape[0]
    column = lax.broadcasted_iota(jnp.int32, (8, half), 1) + lax.axis_index("row") * half
    live = jnp.where(column < count, 1.0, 0.0).astype(f32)
    live_ref[...] = live
    masked = basis * live[:1]
    masked_ref[...] = masked * (1.0 - shrink_weight)
    for i, piece in enumerate(split3(basis)):
        split_ref[i * rank : (i + 1) * rank, :] = piece
    gram_ref[...] = dot(masked, masked, NT, HIGHEST)


def project_kernel(
    rank, values_ref, live_ref, split_ref, own_gram_ref, peer_gram_ref,
    standard_ref, part_ref, gram_ref,
):
    values = values_ref[...].astype(f32)
    samples = values.shape[0]
    mean = jnp.sum(values, axis=0, keepdims=True) * (1.0 / samples)
    centered = values - mean
    var = jnp.sum(centered * centered, axis=0, keepdims=True) * (1.0 / samples)
    scale = lax.rsqrt(var + epsilon)
    standard = jnp.where(live_ref[:1] > 0.0, centered * scale, 0.0).astype(bf16)
    standard_ref[...] = standard
    wide = dot(split_ref[...], standard, NT)
    part_ref[:rank, :] = wide[:rank] + (wide[rank : 2 * rank] + wide[2 * rank :])
    part_ref[rank:, :] = dot(standard, standard, NT)
    gram_ref[...] = (own_gram_ref[...] + peer_gram_ref[...]) * (1.0 - shrink_weight) ** 2


def factor_and_inverse(gram, panels):
    rank = gram.shape[0]
    row_ids = lax.broadcasted_iota(jnp.int32, (rank, rank), 0)
    col_ids = lax.broadcasted_iota(jnp.int32, (rank, rank), 1)
    eye = jnp.where(row_ids == col_ids, 1.0, 0.0).astype(f32)
    full = jnp.concatenate([gram, eye], axis=1)
    lanes = 2 * rank
    tiles = rank // 8
    work = [full[8 * t : 8 * t + 8] for t in range(tiles)]
    sublane = lax.broadcasted_iota(jnp.int32, (8, lanes), 0)
    cols = {}

    def row(tile, r):
        return jnp.broadcast_to(tile[r : r + 1, :], (8, lanes))

    for k in range(rank):
        for start, first, last in panels:
            if start == k:
                for j in range(first, last):
                    for t in range(j // 8, tiles):
                        cols[j, t] = jnp.broadcast_to(work[t][:, j : j + 1], (8, lanes))
        t0, r = k // 8, k % 8
        root = lax.rsqrt(row(cols[k, t0], r))
        square = root * root
        mult = {t: cols[k, t] * square for t in range(t0, tiles)}
        mult[t0] = jnp.where(sublane > r, mult[t0], 0.0)
        for j in range(k + 1, rank):
            if (j, tiles - 1) in cols:
                pivot = row(cols[k, j // 8], j % 8)
                for t in range(j // 8, tiles):
                    cols[j, t] = cols[j, t] - mult[t] * pivot
        pivot = row(work[t0], r)
        for t in range(t0, tiles):
            work[t] = work[t] - mult[t] * pivot
            del cols[k, t]
        work[t0] = jnp.where(sublane == r, pivot * root, work[t0])
    whole = jnp.concatenate(work, axis=0)
    upper = jnp.where(row_ids <= col_ids, whole[:, :rank], 0.0)
    return upper.T, whole[:, rank:]


def finish_kernel(
    scale, own_ref, peer_ref, basis_gram_ref, standard_ref, masked_ref,
    image_ref, new_ref, factor_ref, image_buf, new_buf, factor_buf, sems,
):
    rank = masked_ref.shape[0]
    total = own_ref[...] + peer_ref[...]
    proj = total[:rank]
    cross = total[rank:]
    samples = cross.shape[0]
    keep = 1.0 - shrink_weight
    diagonal = lax.broadcasted_iota(jnp.int32, (samples, samples), 0) == lax.broadcasted_iota(
        jnp.int32, (samples, samples), 1
    )
    middle = cross * (scale * scale) + jnp.where(diagonal, 2.0 * scale * keep, 0.0).astype(f32)
    gram = dot(dot(proj, middle, NN, HIGHEST), proj, NT, HIGHEST) + basis_gram_ref[...]
    rows = jnp.concatenate(split3(proj * scale), axis=0)
    wide = dot(rows, standard_ref[...], NN)
    image = wide[:rank] + (wide[rank : 2 * rank] + wide[2 * rank :]) + masked_ref[...]
    image_buf[...] = image
    image_copy = pltpu.make_async_copy(image_buf, image_ref, sems.at[0])
    image_copy.start()
    lower, inverse = factor_and_inverse(gram, PANELS)
    factor_buf[...] = lower
    factor_copy = pltpu.make_async_copy(factor_buf, factor_ref, sems.at[2])
    factor_copy.start()
    new_buf[...] = dot(inverse, image_buf[...], NN, HIGHEST)
    new_copy = pltpu.make_async_copy(new_buf, new_ref, sems.at[1])
    new_copy.start()
    image_copy.wait()
    factor_copy.wait()
    new_copy.wait()


def body(genotypes, assignment, snp_counts, basis):
    samples, blocks, half = genotypes.shape
    owned, rank, _ = basis.shape
    assert owned == 1
    group = 16 if blocks % 16 == 0 else blocks
    limit = 24 * 2**20
    scalars = [pl.BlockSpec(memory_space=SMEM)]
    width = min(half, WIDTH)
    pieces = half // width
    anywhere = [pl.BlockSpec(memory_space=pl.ANY)]
    ordered = pl.pallas_call(
        functools.partial(order_kernel, samples, blocks, group, width),
        out_shape=jax.ShapeDtypeStruct((blocks * samples, half), bf16),
        in_specs=anywhere * 2,
        out_specs=anywhere[0],
        scratch_shapes=[
            pltpu.SMEM((blocks,), jnp.int32),
            pltpu.VMEM((samples * blocks, half), bf16),
            pltpu.VMEM((samples * blocks, half), bf16),
            pltpu.SemaphoreType.DMA,
            pltpu.SemaphoreType.DMA((pieces,)),
            pltpu.SemaphoreType.DMA((pieces,)),
        ],
        name="order",
    )(assignment, genotypes.reshape(samples * blocks, half))
    regrouped = lax.all_to_all(
        ordered.reshape(blocks, samples, half), "blk", split_axis=0, concat_axis=0, tiled=True
    )
    split, masked, live, basis_gram = pl.pallas_call(
        functools.partial(basis_kernel, half),
        out_shape=[
            jax.ShapeDtypeStruct((3 * rank, half), bf16),
            jax.ShapeDtypeStruct((rank, half), f32),
            jax.ShapeDtypeStruct((8, half), f32),
            jax.ShapeDtypeStruct((rank, rank), f32),
        ],
        in_specs=scalars * 2 + in_vmem(1),
        out_specs=in_vmem(4),
        cost_estimate=pl.CostEstimate(flops=2**26, bytes_accessed=2**20, transcendentals=0),
        name="basis", compiler_params=pltpu.CompilerParams(vmem_limit_bytes=limit),
    )(assignment, snp_counts, basis[0])
    swap = [(0, 1), (1, 0)]
    peer_basis_gram = lax.ppermute(basis_gram, "row", swap)
    total = blocks * samples
    standard, part, gram = pl.pallas_call(
        functools.partial(project_kernel, rank),
        out_shape=[
            jax.ShapeDtypeStruct((total, half), bf16),
            jax.ShapeDtypeStruct((rank + total, total), f32),
            jax.ShapeDtypeStruct((rank, rank), f32),
        ],
        in_specs=in_vmem(5),
        out_specs=in_vmem(3),
        name="project", compiler_params=pltpu.CompilerParams(vmem_limit_bytes=limit),
    )(regrouped.reshape(total, half), live, split, basis_gram, peer_basis_gram)
    peer_part = lax.ppermute(part, "row", swap)
    image, new_basis, factor = pl.pallas_call(
        functools.partial(finish_kernel, shrink_weight / total),
        out_shape=[
            jax.ShapeDtypeStruct((rank, half), f32),
            jax.ShapeDtypeStruct((rank, half), f32),
            jax.ShapeDtypeStruct((rank, rank), f32),
        ],
        in_specs=in_vmem(5),
        out_specs=[pl.BlockSpec(memory_space=pl.ANY)] * 3,
        scratch_shapes=[
            pltpu.VMEM((rank, half), f32),
            pltpu.VMEM((rank, half), f32),
            pltpu.VMEM((rank, rank), f32),
            pltpu.SemaphoreType.DMA((3,)),
        ],
        name="finish", compiler_params=pltpu.CompilerParams(vmem_limit_bytes=limit),
    )(part, peer_part, gram, standard, masked)
    return image[None], new_basis[None], factor[None]


def solution(mesh):
    in_specs = (P("blk", None, "row"), P(), P(), P("blk", None, "row"))
    out_specs = (P("blk", None, "row"), P("blk", None, "row"), P("blk", None, None))
    return jax.shard_map(body, mesh=mesh, in_specs=in_specs, out_specs=out_specs, check_vma=False)
```

time: 31.3 us -> 26.8 us (0.86)
  Pallas kernels: 11.2 us -> 7.02 us
  local copies, waits for them, and re-layouts: 1.35 us -> 0.65 us
  waiting for transfers between devices: 8.95 us -> 9.46 us
    pallas_call x1, Pallas kernels: 5.21 us -> 3.42 us  [body(): pl.pallas_call(functools.partial(finish_kernel, shrink_weight / total), o...]
    pallas_call x1, Pallas kernels: 2.18 us -> 0.44 us  [body(): pl.pallas_call(functools.partial(project_kernel, rank), out_shape=[jax.Sh...]
    ppermute x1, waiting for transfers between devices: 0.01 us -> 1.29 us  [body(): peer_part = lax.ppermute(part, 'row', swap)]
    pallas_call x1, Pallas kernels: 1.97 us -> 0.94 us  [body(): pl.pallas_call(functools.partial(basis_kernel, half), out_shape=[jax.Shap...]
    all_to_all x1, waiting for transfers between devices: 7.9 us -> 6.98 us  [body(): lax.all_to_all(ordered.reshape(blocks, samples, half), 'blk', split_axis=...]
    unnamed x8 -> x6, local copies, waits for them, and re-layouts: 1.35 us -> 0.65 us
    ppermute x1, starting transfers between devices: 0.51 us -> 0.07 us  [body(): peer_basis_gram = lax.ppermute(basis_gram, 'row', swap)]
    pallas_call x1, Pallas kernels: 1.88 us -> 2.22 us  [body(): pl.pallas_call(functools.partial(order_kernel, samples, blocks, group, wi...]
  transfers between devices with their start and end apart: 3 -> 3, of which waited for: 2 -> 3; matrix products, arithmetic and copies ran while one was open for 0% -> 0% of each run, Pallas kernels for 6% -> 4%
where the time goes in v2:
time: 26.8 us; the launch traced here: 26.5 us
  waiting for transfers between devices  9.46 us (35%)
  starting transfers between devices  8.63 us (32%)
  Pallas kernels  7.02 us (26%)
  between operations  0.71 us (3%)
  local copies, waits for them, and re-layouts  0.65 us (2%)
    all_to_all x1, starting transfers between devices, body(): lax.all_to_all(ordered.reshape(blocks, samples, half), 'blk', split_axis=...  8.48 us
    all_to_all x1, waiting for transfers between devices, body(): lax.all_to_all(ordered.reshape(blocks, samples, half), 'blk', split_axis=...  6.98 us
    pallas_call x1, Pallas kernels, body(): pl.pallas_call(functools.partial(finish_kernel, shrink_weight / total), o...  3.42 us
    pallas_call x1, Pallas kernels, body(): pl.pallas_call(functools.partial(order_kernel, samples, blocks, group, wi...  2.22 us
    ppermute x1, waiting for transfers between devices, body(): peer_part = lax.ppermute(part, 'row', swap)  1.29 us
    ppermute x1, waiting for transfers between devices, body(): peer_basis_gram = lax.ppermute(basis_gram, 'row', swap)  1.19 us
    pallas_call x1, Pallas kernels, body(): pl.pallas_call(functools.partial(basis_kernel, half), out_shape=[jax.Shap...  0.94 us
    unnamed x6, local copies, waits for them, and re-layouts  0.65 us
  transfers between devices with their start and end apart: 3, of which 3 were waited for; matrix products, arithmetic and copies ran while one was open for 0% of the time, Pallas kernels for 4%

profile of v2, /device:TPU:0, one launch (start us, length us, event | category | flops | bytes accessed | tf_op | source)
XLA Modules:
  0.0 26.5 jit_solution(17912206205319004184)
XLA Ops:
  0.6 2.2 %order.1 = bf16[128,1024]{1,0:T(8,128)(2,1)} custom-call(s32[16]{0:T(128)} %assignment.1, bf16[128,1024]{1,0:T(8,128)(2,1)} %bitcast.10), custom_call_target="tpu_custom_call" | custom-call | tf_op jit(solution)/shard_map/order/pallas_call | solution.py:197
  2.9 0.0 copy-start
  2.9 8.5 %all-to-all-start = ((bf16[16,8,1024]{2,1,0:T(8,128)(2,1)}), bf16[16,8,1024]{2,1,0:T(8,128)(2,1)S(1)}, u32[]{:S(2)}, u32[]{:S(2)}) async-start(bf16[16,8,1024]{2,1,0:T(8,128)(2,1)} %bitcast.9), calls=%async_computation | async-start | bytes 524288 | tf_op jit(solution)/shard_map/all_to_all | solution.py:212
  11.4 0.0 copy-start.1
  11.4 0.0 copy-start.2
  11.4 0.0 copy-done
  11.4 0.6 %copy-done.1 = s32[16]{0:T(128)S(1)} copy-done((s32[16]{0:T(128)S(1)}, s32[16]{0:T(128)}, u32[]{:S(2)}) %copy-start.1) | copy-done | bytes 88
  12.0 0.0 copy-done.2
  12.0 0.9 %basis.1 = (bf16[192,1024]{1,0:T(8,128)(2,1)S(1)}, f32[64,1024]{1,0:T(8,128)S(1)}, f32[8,1024]{1,0:T(8,128)S(1)}, f32[64,64]{1,0:T(8,128)S(1)}) custom-call(s32[16]{0:T(128)S(1)} %copy-done.1, s32[16]{0:T(128)S(1)} %copy-done.2, f32[64,1024]{1,0:T(8,128)S(1)} %bitcast.8), custom_call_target="tpu_custom_call" | custom-call | flops 67108864 | bytes 1048576 | tf_op jit(solution)/shard_map/basis/pallas_call | solution.py:215
  13.0 0.1 collective-permute-start
  13.1 1.2 %collective-permute-done.peer_gram_ref = f32[64,64]{1,0:T(8,128)S(1)} collective-permute-done((f32[64,64]{1,0:T(8,128)S(1)}, f32[64,64]{1,0:T(8,128)S(1)}, u32[]{:S(2)}, u32[]{:S(2)}) %collective-permute-start) | collective-permute-done | bytes 16416 | tf_op jit(solution)/shard_map/ppermute | solution.py:229
  14.3 7.0 %all-to-all-done = bf16[16,8,1024]{2,1,0:T(8,128)(2,1)S(1)} async-done(((bf16[16,8,1024]{2,1,0:T(8,128)(2,1)}), bf16[16,8,1024]{2,1,0:T(8,128)(2,1)S(1)}, u32[]{:S(2)}, u32[]{:S(2)}) %all-to-all-start) | async-done | bytes 262176 | tf_op jit(solution)/shard_map/all_to_all | solution.py:212
  21.2 0.4 %project.1 = (bf16[128,1024]{1,0:T(8,128)(2,1)S(1)}, f32[192,128]{1,0:T(8,128)S(1)}, f32[64,64]{1,0:T(8,128)S(1)}) custom-call(bf16[128,1024]{1,0:T(8,128)(2,1)S(1)} %bitcast.7, f32[8,1024]{1,0:T(8,128)S(1)} %get-tuple-element.13.live_ref, bf16[192,1024]{1,0:T(8,128)(2,1)S(1)} %get-tuple-element.14.split_ref, f32[64,64]{1,0:T(8,128)S(1)} %get-tuple-element.15.own_gram_ref, ...), custom_call_target="tpu_custom_call" | custom-call | tf_op jit(solution)/shard_map/project/pallas_call | solution.py:231
  21.7 0.1 collective-permute-start.1
  21.8 1.3 %collective-permute-done.1.peer_ref = f32[192,128]{1,0:T(8,128)S(1)} collective-permute-done((f32[192,128]{1,0:T(8,128)S(1)}, f32[192,128]{1,0:T(8,128)S(1)}, u32[]{:S(2)}, u32[]{:S(2)}) %collective-permute-start.1) | collective-permute-done | bytes 98336 | tf_op jit(solution)/shard_map/ppermute | solution.py:242
  23.0 3.4 %finish.1 = (f32[64,1024]{1,0:T(8,128)}, f32[64,1024]{1,0:T(8,128)}, f32[64,64]{1,0:T(8,128)}) custom-call(f32[192,128]{1,0:T(8,128)S(1)} %get-tuple-element.16.own_ref, f32[192,128]{1,0:T(8,128)S(1)} %collective-permute-done.1.peer_ref, f32[64,64]{1,0:T(8,128)S(1)} %get-tuple-element.17.basis_gram_ref, ...), custom_call_target="tpu_custom_call" | custom-call | tf_op jit(solution)/shard_map/finish/pallas_call | solution.py:243
Async XLA Ops:
  2.9 8.5 %copy-start = (f32[1,64,1024]{2,1,0:T(8,128)S(1)}, f32[1,64,1024]{2,1,0:T(8,128)}, u32[]{:S(2)}) copy-start(f32[1,64,1024]{2,1,0:T(8,128)} %param.7) | copy-start | bytes 786436
  2.9 18.4 %all-to-all-start = ((bf16[16,8,1024]{2,1,0:T(8,128)(2,1)}), bf16[16,8,1024]{2,1,0:T(8,128)(2,1)S(1)}, u32[]{:S(2)}, u32[]{:S(2)}) async-start(bf16[16,8,1024]{2,1,0:T(8,128)(2,1)} %bitcast.9), calls=%async_computation | async-start | bytes 524288 | tf_op jit(solution)/shard_map/all_to_all | solution.py:212
  11.4 0.7 %copy-start.1 = (s32[16]{0:T(128)S(1)}, s32[16]{0:T(128)}, u32[]{:S(2)}) copy-start(s32[16]{0:T(128)} %assignment.1) | copy-start | bytes 196
  11.4 0.7 %copy-start.2 = (s32[16]{0:T(128)S(1)}, s32[16]{0:T(128)}, u32[]{:S(2)}) copy-start(s32[16]{0:T(128)} %snp_counts.1) | copy-start | bytes 196
  13.0 1.3 %collective-permute-start = (f32[64,64]{1,0:T(8,128)S(1)}, f32[64,64]{1,0:T(8,128)S(1)}, u32[]{:S(2)}, u32[]{:S(2)}) collective-permute-start(f32[64,64]{1,0:T(8,128)S(1)} %get-tuple-element.15.own_gram_ref), channel_id=1, source_target_pairs={{0,1},{1,0},{2,3},{3,2},{4,5},{5,4},{6,7},{7,6},{8,9},{9,8},{10,11... | collective-permute-start | bytes 49160 | tf_op jit(solution)/shard_map/ppermute | solution.py:229
  21.7 1.4 %collective-permute-start.1 = (f32[192,128]{1,0:T(8,128)S(1)}, f32[192,128]{1,0:T(8,128)S(1)}, u32[]{:S(2)}, u32[]{:S(2)}) collective-permute-start(f32[192,128]{1,0:T(8,128)S(1)} %get-tuple-element.16.own_ref), channel_id=1, source_target_pairs={{0,1},{1,0},{2,3},{3,2},{4,5},{5,4},{6,7},{7,6},{8,9},{9,8},{10,11... | collective-permute-start | bytes 294920 | tf_op jit(solution)/shard_map/ppermute | solution.py:242

commit v3 on v2

v3 whole, which is shorter than its diff:
```python
import functools

import jax
import jax.numpy as jnp
from jax import lax
from jax.experimental import pallas as pl
from jax.experimental.pallas import tpu as pltpu
from jax.sharding import PartitionSpec as P

epsilon = 1e-05
PANELS = tuple((f, f, f + 8) for f in range(0, 64, 8))
shrink_weight = 0.5

VMEM = pltpu.VMEM
SMEM = pltpu.SMEM
HIGHEST = lax.Precision.HIGHEST
f32 = jnp.float32
bf16 = jnp.bfloat16


def dot(x, y, dims, precision=None):
    return lax.dot_general(x, y, (dims, ((), ())), precision=precision, preferred_element_type=f32)


NN = ((1,), (0,))
NT = ((1,), (1,))


def in_vmem(n):
    return [pl.BlockSpec(memory_space=VMEM)] * n


def split3(x):
    high = x.astype(bf16)
    rest = x - high.astype(f32)
    mid = rest.astype(bf16)
    low = (rest - mid.astype(f32)).astype(bf16)
    return high, mid, low


def order_kernel(
    samples, blocks, group, half, assignment_ref, counts_ref, rows_ref, out_ref, live_ref,
    assignment, counts, rows, sems,
):
    fetches = [
        pltpu.make_async_copy(assignment_ref, assignment, sems.at[0]),
        pltpu.make_async_copy(counts_ref, counts, sems.at[1]),
        pltpu.make_async_copy(rows_ref, rows, sems.at[2]),
    ]
    for fetch in fetches:
        fetch.start()
    shape = (samples, samples * blocks)
    column = lax.broadcasted_iota(jnp.int32, shape, 1)
    start = lax.broadcasted_iota(jnp.int32, shape, 0) * blocks
    position = lax.broadcasted_iota(jnp.int32, (8, half), 1) + lax.axis_index("row") * half
    fetches[0].wait()
    picks = []
    for first in range(0, blocks, group):
        ones = [
            jnp.where(column == start + assignment[first + s], 1.0, 0.0).astype(f32)
            for s in range(group)
        ]
        picks.append(jnp.concatenate(ones, axis=0).astype(bf16))
    fetches[1].wait()
    count = counts[assignment[lax.axis_index("blk")]]
    live_ref[...] = jnp.where(position < count, 1.0, 0.0).astype(f32)
    fetches[2].wait()
    for g, pick in enumerate(picks):
        span = slice(g * group * samples, (g + 1) * group * samples)
        out_ref[span, :] = dot(pick, rows[...], NN).astype(bf16)


def project_kernel(values_ref, live_ref, basis_ref, standard_ref, masked_ref, part_ref):
    live = live_ref[:1]
    masked = basis_ref[...] * live
    rank = masked.shape[0]
    masked_ref[...] = masked * (1.0 - shrink_weight)
    high, mid, low = split3(masked)
    values = values_ref[...].astype(f32)
    samples = values.shape[0]
    mean = jnp.sum(values, axis=0, keepdims=True) * (1.0 / samples)
    centered = values - mean
    var = jnp.sum(centered * centered, axis=0, keepdims=True) * (1.0 / samples)
    scale = lax.rsqrt(var + epsilon)
    standard = jnp.where(live > 0.0, centered * scale, 0.0).astype(bf16)
    standard_ref[...] = standard
    left = jnp.concatenate([high, mid, low, standard], axis=0)
    right = jnp.concatenate([standard, high, mid], axis=0)
    wide = dot(left, right, NT)
    part_ref[:rank, :] = wide[:rank, :samples] + (
        wide[rank : 2 * rank, :samples] + wide[2 * rank : 3 * rank, :samples]
    )
    part_ref[rank : rank + samples, :] = wide[3 * rank :, :samples]
    at_high = slice(samples, samples + rank)
    at_mid = slice(samples + rank, samples + 2 * rank)
    even = wide[:rank, at_high] + wide[rank : 2 * rank, at_mid]
    odd = wide[rank : 2 * rank, at_high] + wide[2 * rank : 3 * rank, at_high]
    part_ref[rank + samples :, : 2 * rank] = jnp.concatenate([even, odd], axis=1)


def factor_and_inverse(gram, panels):
    rank = gram.shape[0]
    row_ids = lax.broadcasted_iota(jnp.int32, (rank, rank), 0)
    col_ids = lax.broadcasted_iota(jnp.int32, (rank, rank), 1)
    eye = jnp.where(row_ids == col_ids, 1.0, 0.0).astype(f32)
    full = jnp.concatenate([gram, eye], axis=1)
    lanes = 2 * rank
    tiles = rank // 8
    work = [full[8 * t : 8 * t + 8] for t in range(tiles)]
    sublane = lax.broadcasted_iota(jnp.int32, (8, lanes), 0)
    cols = {}

    def row(tile, r):
        return jnp.broadcast_to(tile[r : r + 1, :], (8, lanes))

    for k in range(rank):
        for start, first, last in panels:
            if start == k:
                for j in range(first, last):
                    for t in range(j // 8, tiles):
                        cols[j, t] = jnp.broadcast_to(work[t][:, j : j + 1], (8, lanes))
        t0, r = k // 8, k % 8
        root = lax.rsqrt(row(cols[k, t0], r))
        square = root * root
        mult = {t: cols[k, t] * square for t in range(t0, tiles)}
        mult[t0] = jnp.where(sublane > r, mult[t0], 0.0)
        for j in range(k + 1, rank):
            if (j, tiles - 1) in cols:
                pivot = row(cols[k, j // 8], j % 8)
                for t in range(j // 8, tiles):
                    cols[j, t] = cols[j, t] - mult[t] * pivot
        pivot = row(work[t0], r)
        for t in range(t0, tiles):
            work[t] = work[t] - mult[t] * pivot
            del cols[k, t]
        work[t0] = jnp.where(sublane == r, pivot * root, work[t0])
    whole = jnp.concatenate(work, axis=0)
    upper = jnp.where(row_ids <= col_ids, whole[:, :rank], 0.0)
    return upper.T, whole[:, rank:]


def finish_kernel(
    scale, own_ref, peer_ref, standard_ref, masked_ref,
    image_ref, new_ref, factor_ref, image_buf, new_buf, factor_buf, sems,
):
    rank = masked_ref.shape[0]
    total = own_ref[...] + peer_ref[...]
    proj = total[:rank]
    samples = total.shape[1]
    cross = total[rank : rank + samples]
    even = total[rank + samples :, :rank]
    odd = total[rank + samples :, rank : 2 * rank]
    basis_gram = even + (odd + odd.T)
    keep = 1.0 - shrink_weight
    diagonal = lax.broadcasted_iota(jnp.int32, (samples, samples), 0) == lax.broadcasted_iota(
        jnp.int32, (samples, samples), 1
    )
    middle = cross * (scale * scale) + jnp.where(diagonal, 2.0 * scale * keep, 0.0).astype(f32)
    gram = dot(dot(proj, middle, NN, HIGHEST), proj, NT, HIGHEST)
    gram = gram + basis_gram * (keep * keep)
    rows = jnp.concatenate(split3(proj * scale), axis=0)
    wide = dot(rows, standard_ref[...], NN)
    image = wide[:rank] + (wide[rank : 2 * rank] + wide[2 * rank :]) + masked_ref[...]
    image_buf[...] = image
    image_copy = pltpu.make_async_copy(image_buf, image_ref, sems.at[0])
    image_copy.start()
    lower, inverse = factor_and_inverse(gram, PANELS)
    factor_buf[...] = lower
    factor_copy = pltpu.make_async_copy(factor_buf, factor_ref, sems.at[2])
    factor_copy.start()
    new_buf[...] = dot(inverse, image_buf[...], NN, HIGHEST)
    new_copy = pltpu.make_async_copy(new_buf, new_ref, sems.at[1])
    new_copy.start()
    image_copy.wait()
    factor_copy.wait()
    new_copy.wait()


def body(genotypes, assignment, snp_counts, basis):
    samples, blocks, half = genotypes.shape
    owned, rank, _ = basis.shape
    assert owned == 1
    group = 16 if blocks % 16 == 0 else blocks
    limit = 24 * 2**20
    params = pltpu.CompilerParams(vmem_limit_bytes=limit)
    anywhere = [pl.BlockSpec(memory_space=pl.ANY)]
    ordered, live = pl.pallas_call(
        functools.partial(order_kernel, samples, blocks, group, half),
        out_shape=[
            jax.ShapeDtypeStruct((blocks * samples, half), bf16),
            jax.ShapeDtypeStruct((8, half), f32),
        ],
        in_specs=[pl.BlockSpec(memory_space=pltpu.HBM)] * 3,
        out_specs=in_vmem(2),
        scratch_shapes=[
            pltpu.SMEM((blocks,), jnp.int32),
            pltpu.SMEM((blocks,), jnp.int32),
            pltpu.VMEM((samples * blocks, half), bf16),
            pltpu.SemaphoreType.DMA((3,)),
        ],
        compiler_params=params,
        name="order",
    )(*[
        pltpu.with_memory_space_constraint(x, pltpu.HBM)
        for x in (assignment, snp_counts, genotypes.reshape(samples * blocks, half))
    ])
    regrouped = lax.all_to_all(
        ordered.reshape(blocks, samples, half), "blk", split_axis=0, concat_axis=0, tiled=True
    )
    total = blocks * samples
    standard, masked, part = pl.pallas_call(
        project_kernel,
        out_shape=[
            jax.ShapeDtypeStruct((total, half), bf16),
            jax.ShapeDtypeStruct((rank, half), f32),
            jax.ShapeDtypeStruct((2 * rank + total, total), f32),
        ],
        in_specs=in_vmem(3),
        out_specs=in_vmem(3),
        compiler_params=params,
        name="project",
    )(regrouped.reshape(total, half), live, basis[0])
    peer_part = lax.ppermute(part, "row", [(0, 1), (1, 0)])
    image, new_basis, factor = pl.pallas_call(
        functools.partial(finish_kernel, shrink_weight / total),
        out_shape=[
            jax.ShapeDtypeStruct((rank, half), f32),
            jax.ShapeDtypeStruct((rank, half), f32),
            jax.ShapeDtypeStruct((rank, rank), f32),
        ],
        in_specs=in_vmem(4),
        out_specs=anywhere * 3,
        scratch_shapes=[
            pltpu.VMEM((rank, half), f32),
            pltpu.VMEM((rank, half), f32),
            pltpu.VMEM((rank, rank), f32),
            pltpu.SemaphoreType.DMA((3,)),
        ],
        compiler_params=params,
        name="finish",
    )(part, peer_part, standard, masked)
    return image[None], new_basis[None], factor[None]


def solution(mesh):
    in_specs = (P("blk", None, "row"), P(), P(), P("blk", None, "row"))
    out_specs = (P("blk", None, "row"), P("blk", None, "row"), P("blk", None, None))
    return jax.shard_map(body, mesh=mesh, in_specs=in_specs, out_specs=out_specs, check_vma=False)
```

time: 26.8 us -> 25.7 us (0.959)
  blocking collectives: 0 us -> 18.1 us
  starting transfers between devices: 8.63 us -> 0.07 us
  waiting for transfers between devices: 9.46 us -> 1.33 us
  Pallas kernels: 7.02 us -> 5.29 us
  local copies, waits for them, and re-layouts: 0.65 us -> 0.01 us
    all_to_all x0 -> x1, blocking collectives: none -> 18.1 us  [body(): lax.all_to_all(ordered.reshape(blocks, samples, half), 'blk', split_axis=...]
    all_to_all x1 -> x0, starting transfers between devices: 8.48 us -> none  [body(): lax.all_to_all(ordered.reshape(blocks, samples, half), 'blk', split_axis=...]
    all_to_all x1 -> x0, waiting for transfers between devices: 6.98 us -> none  [body(): lax.all_to_all(ordered.reshape(blocks, samples, half), 'blk', split_axis=...]
    pallas_call x3 -> x2, Pallas kernels: 3.6 us -> 1.74 us  [the longest x1 1.19 us: body(): pl.pallas_call(functools.partial(order_kernel, samples, blocks, group, ha...]
    ppermute x2 -> x1, waiting for transfers between devices: 2.48 us -> 1.33 us  [body(): peer_part = lax.ppermute(part, 'row', [(0, 1), (1, 0)])]
    unnamed x6 -> x2, local copies, waits for them, and re-layouts: 0.65 us -> 0.01 us
  transfers between devices with their start and end apart: 3 -> 1, of which waited for: 3 -> 1; matrix products, arithmetic and copies ran while one was open for 0% -> 0% of each run, Pallas kernels for 4% -> 0%
where the time goes in v3:
time: 25.7 us; the launch traced here: 25.5 us
  blocking collectives  18.1 us (70%)
  Pallas kernels  5.29 us (21%)
  waiting for transfers between devices  1.33 us (5%)
  between operations  0.66 us (3%)
    all_to_all x1, blocking collectives, body(): lax.all_to_all(ordered.reshape(blocks, samples, half), 'blk', split_axis=...  18.1 us
    pallas_call x1, Pallas kernels, body(): pl.pallas_call(functools.partial(finish_kernel, shrink_weight / total), o...  3.55 us
    ppermute x1, waiting for transfers between devices, body(): peer_part = lax.ppermute(part, 'row', [(0, 1), (1, 0)])  1.33 us
    pallas_call x1, Pallas kernels, body(): pl.pallas_call(functools.partial(order_kernel, samples, blocks, group, ha...  1.19 us
    pallas_call x1, Pallas kernels, body(): pl.pallas_call(project_kernel, out_shape=[jax.ShapeDtypeStruct((total, ha...  0.54 us
  transfers between devices with their start and end apart: 1, of which 1 were waited for; matrix products, arithmetic and copies ran while one was open for 0% of the time, Pallas kernels for 0%

profile of v3, /device:TPU:0, one launch (start us, length us, event | category | flops | bytes accessed | tf_op | source)
XLA Modules:
  0.0 25.5 jit_solution(12733342734643490390)
XLA Ops:
  0.6 1.2 %order.1 = (bf16[128,1024]{1,0:T(8,128)(2,1)S(1)}, f32[8,1024]{1,0:T(8,128)S(1)}) custom-call(s32[16]{0:T(128)} %assignment_ref.1, s32[16]{0:T(128)} %counts_ref.1, bf16[128,1024]{1,0:T(8,128)(2,1)} %bitcast.10), custom_call_target="tpu_custom_call" | custom-call | tf_op jit(solution)/shard_map/order/pallas_call | solution.py:187
  1.8 0.0 copy-start
  1.8 18.1 %all_to_all.5 = bf16[16,8,1024]{2,1,0:T(8,128)(2,1)S(1)} all-to-all(bf16[16,8,1024]{2,1,0:T(8,128)(2,1)S(1)} %bitcast.9), channel_id=1, replica_groups=mesh['blk'=16,'row'=2] {'blk'}, dimensions={0} | all-to-all | bytes 524288 | tf_op jit(solution)/shard_map/all_to_all | solution.py:207
  20.0 0.0 copy-done
  20.0 0.5 %project.1 = (bf16[128,1024]{1,0:T(8,128)(2,1)S(1)}, f32[64,1024]{1,0:T(8,128)S(1)}, f32[256,128]{1,0:T(8,128)S(1)}) custom-call(bf16[128,1024]{1,0:T(8,128)(2,1)S(1)} %bitcast.7, f32[8,1024]{1,0:T(8,128)S(1)} %get-tuple-element.12.live_ref, f32[64,1024]{1,0:T(8,128)S(1)} %bitcast.8), custom_call_target="tpu_custom_call" | custom-call | tf_op jit(solution)/shard_map/project/pallas_call | solution.py:211
  20.5 0.1 collective-permute-start
  20.6 1.3 %collective-permute-done.peer_ref = f32[256,128]{1,0:T(8,128)S(1)} collective-permute-done((f32[256,128]{1,0:T(8,128)S(1)}, f32[256,128]{1,0:T(8,128)S(1)}, u32[]{:S(2)}, u32[]{:S(2)}) %collective-permute-start) | collective-permute-done | bytes 131104 | tf_op jit(solution)/shard_map/ppermute | solution.py:223
  21.9 3.6 %finish.1 = (f32[64,1024]{1,0:T(8,128)}, f32[64,1024]{1,0:T(8,128)}, f32[64,64]{1,0:T(8,128)}) custom-call(f32[256,128]{1,0:T(8,128)S(1)} %get-tuple-element.13.own_ref, f32[256,128]{1,0:T(8,128)S(1)} %collective-permute-done.peer_ref, bf16[128,1024]{1,0:T(8,128)(2,1)S(1)} %get-tuple-element.14.standard_ref, f32[64,1024]{1,0:T(8,128)S(1)} %get-tuple-element.15.masked_ref), custom_call_target="tpu_custom_call" | custom-call | tf_op jit(solution)/shard_map/finish/pallas_call | solution.py:224
Async XLA Ops:
  1.8 18.2 %copy-start = (f32[1,64,1024]{2,1,0:T(8,128)S(1)}, f32[1,64,1024]{2,1,0:T(8,128)}, u32[]{:S(2)}) copy-start(f32[1,64,1024]{2,1,0:T(8,128)} %param.7) | copy-start | bytes 786436
  20.5 1.4 %collective-permute-start = (f32[256,128]{1,0:T(8,128)S(1)}, f32[256,128]{1,0:T(8,128)S(1)}, u32[]{:S(2)}, u32[]{:S(2)}) collective-permute-start(f32[256,128]{1,0:T(8,128)S(1)} %get-tuple-element.13.own_ref), channel_id=1, source_target_pairs={{0,1},{1,0},{2,3},{3,2},{4,5},{5,4},{6,7},{7,6},{8,9},{9,8},{10,11... | collective-permute-start | bytes 393224 | tf_op jit(solution)/shard_map/ppermute | solution.py:223

commit v4 on v3

--- a/solution.py
+++ b/solution.py
@@ -8,7 +8,7 @@
 from jax.sharding import PartitionSpec as P
 
 epsilon = 1e-05
-PANELS = tuple((f, f, f + 8) for f in range(0, 64, 8))
+PANELS = tuple((max(f - 4, 0), f, f + 4) for f in range(0, 64, 4))
 shrink_weight = 0.5
 
 VMEM = pltpu.VMEM
@@ -118,7 +118,7 @@
             if start == k:
                 for j in range(first, last):
                     for t in range(j // 8, tiles):
-                        cols[j, t] = jnp.broadcast_to(work[t][:, j : j + 1], (8, lanes))
+                        cols[j, t] = jnp.take_along_axis(work[t], jnp.full((8, lanes), j, jnp.int32), axis=1)
         t0, r = k // 8, k % 8
         root = lax.rsqrt(row(cols[k, t0], r))
         square = root * root
@@ -136,12 +136,13 @@
         work[t0] = jnp.where(sublane == r, pivot * root, work[t0])
     whole = jnp.concatenate(work, axis=0)
     upper = jnp.where(row_ids <= col_ids, whole[:, :rank], 0.0)
-    return upper.T, whole[:, rank:]
+    lane = lax.broadcasted_iota(jnp.int32, (rank, lanes), 1)
+    return upper.T, jnp.where(lane >= rank, whole, 0.0)
 
 
 def finish_kernel(
     scale, own_ref, peer_ref, standard_ref, masked_ref,
-    image_ref, new_ref, factor_ref, image_buf, new_buf, factor_buf, sems,
+    image_ref, new_ref, factor_ref, image_buf, new_buf, factor_buf, stack, sems,
 ):
     rank = masked_ref.shape[0]
     total = own_ref[...] + peer_ref[...]
@@ -164,13 +165,23 @@
     image_buf[...] = image
     image_copy = pltpu.make_async_copy(image_buf, image_ref, sems.at[0])
     image_copy.start()
+    high = image.astype(bf16)
+    mid = (image - high.astype(f32)).astype(bf16)
+    for i, piece in enumerate((high, high, high, mid)):
+        stack[i * rank : (i + 1) * rank, :] = piece
     lower, inverse = factor_and_inverse(gram, PANELS)
+    high = inverse.astype(bf16)
+    mid = (inverse - high.astype(f32)).astype(bf16)
+    left = jnp.concatenate(
+        [jnp.concatenate([high, high], axis=1), jnp.concatenate([mid, mid], axis=1)], axis=0
+    )
+    wide = dot(left, stack[...], NN)
+    new_buf[...] = wide[:rank] + wide[rank:]
+    new_copy = pltpu.make_async_copy(new_buf, new_ref, sems.at[1])
+    new_copy.start()
     factor_buf[...] = lower
     factor_copy = pltpu.make_async_copy(factor_buf, factor_ref, sems.at[2])
     factor_copy.start()
-    new_buf[...] = dot(inverse, image_buf[...], NN, HIGHEST)
-    new_copy = pltpu.make_async_copy(new_buf, new_ref, sems.at[1])
-    new_copy.start()
     image_copy.wait()
     factor_copy.wait()
     new_copy.wait()
@@ -234,6 +245,7 @@
             pltpu.VMEM((rank, half), f32),
             pltpu.VMEM((rank, half), f32),
             pltpu.VMEM((rank, rank), f32),
+            pltpu.VMEM((4 * rank, half), bf16),
             pltpu.SemaphoreType.DMA((3,)),
         ],
         compiler_params=params,

time: 25.7 us -> 24.8 us (0.965)
  Pallas kernels: 5.29 us -> 4.44 us
    pallas_call x1, Pallas kernels: 3.55 us -> 2.7 us  [body(): pl.pallas_call(functools.partial(finish_kernel, shrink_weight / total), o...]
where the time goes in v4:
time: 24.8 us; the launch traced here: 24.7 us
  blocking collectives  18.1 us (73%)
  Pallas kernels  4.44 us (18%)
  waiting for transfers between devices  1.33 us (5%)
  between operations  0.66 us (3%)
    all_to_all x1, blocking collectives, body(): lax.all_to_all(ordered.reshape(blocks, samples, half), 'blk', split_axis=...  18.1 us
    pallas_call x1, Pallas kernels, body(): pl.pallas_call(functools.partial(finish_kernel, shrink_weight / total), o...  2.7 us
    ppermute x1, waiting for transfers between devices, body(): peer_part = lax.ppermute(part, 'row', [(0, 1), (1, 0)])  1.33 us
    pallas_call x1, Pallas kernels, body(): pl.pallas_call(functools.partial(order_kernel, samples, blocks, group, ha...  1.19 us
    pallas_call x1, Pallas kernels, body(): pl.pallas_call(project_kernel, out_shape=[jax.ShapeDtypeStruct((total, ha...  0.54 us
  transfers between devices with their start and end apart: 1, of which 1 were waited for; matrix products, arithmetic and copies ran while one was open for 0% of the time, Pallas kernels for 0%

profile of v4, /device:TPU:0, one launch (start us, length us, event | category | flops | bytes accessed | tf_op | source)
XLA Modules:
  0.0 24.7 jit_solution(16039739656288586934)
XLA Ops:
  0.6 1.2 %order.1 = (bf16[128,1024]{1,0:T(8,128)(2,1)S(1)}, f32[8,1024]{1,0:T(8,128)S(1)}) custom-call(s32[16]{0:T(128)} %assignment_ref.1, s32[16]{0:T(128)} %counts_ref.1, bf16[128,1024]{1,0:T(8,128)(2,1)} %bitcast.10), custom_call_target="tpu_custom_call" | custom-call | tf_op jit(solution)/shard_map/order/pallas_call | solution.py:198
  1.8 0.0 copy-start
  1.8 18.1 %all_to_all.5 = bf16[16,8,1024]{2,1,0:T(8,128)(2,1)S(1)} all-to-all(bf16[16,8,1024]{2,1,0:T(8,128)(2,1)S(1)} %bitcast.9), channel_id=1, replica_groups=mesh['blk'=16,'row'=2] {'blk'}, dimensions={0} | all-to-all | bytes 524288 | tf_op jit(solution)/shard_map/all_to_all | solution.py:218
  20.0 0.0 copy-done
  20.0 0.5 %project.1 = (bf16[128,1024]{1,0:T(8,128)(2,1)S(1)}, f32[64,1024]{1,0:T(8,128)S(1)}, f32[256,128]{1,0:T(8,128)S(1)}) custom-call(bf16[128,1024]{1,0:T(8,128)(2,1)S(1)} %bitcast.7, f32[8,1024]{1,0:T(8,128)S(1)} %get-tuple-element.12.live_ref, f32[64,1024]{1,0:T(8,128)S(1)} %bitcast.8), custom_call_target="tpu_custom_call" | custom-call | tf_op jit(solution)/shard_map/project/pallas_call | solution.py:222
  20.5 0.1 collective-permute-start
  20.6 1.3 %collective-permute-done.peer_ref = f32[256,128]{1,0:T(8,128)S(1)} collective-permute-done((f32[256,128]{1,0:T(8,128)S(1)}, f32[256,128]{1,0:T(8,128)S(1)}, u32[]{:S(2)}, u32[]{:S(2)}) %collective-permute-start) | collective-permute-done | bytes 131104 | tf_op jit(solution)/shard_map/ppermute | solution.py:234
  21.9 2.7 %finish.1 = (f32[64,1024]{1,0:T(8,128)}, f32[64,1024]{1,0:T(8,128)}, f32[64,64]{1,0:T(8,128)}) custom-call(f32[256,128]{1,0:T(8,128)S(1)} %get-tuple-element.13.own_ref, f32[256,128]{1,0:T(8,128)S(1)} %collective-permute-done.peer_ref, bf16[128,1024]{1,0:T(8,128)(2,1)S(1)} %get-tuple-element.14.standard_ref, f32[64,1024]{1,0:T(8,128)S(1)} %get-tuple-element.15.masked_ref), custom_call_target="tpu_custom_call" | custom-call | tf_op jit(solution)/shard_map/finish/pallas_call | solution.py:235
Async XLA Ops:
  1.8 18.2 %copy-start = (f32[1,64,1024]{2,1,0:T(8,128)S(1)}, f32[1,64,1024]{2,1,0:T(8,128)}, u32[]{:S(2)}) copy-start(f32[1,64,1024]{2,1,0:T(8,128)} %param.7) | copy-start | bytes 786436
  20.5 1.4 %collective-permute-start = (f32[256,128]{1,0:T(8,128)S(1)}, f32[256,128]{1,0:T(8,128)S(1)}, u32[]{:S(2)}, u32[]{:S(2)}) collective-permute-start(f32[256,128]{1,0:T(8,128)S(1)} %get-tuple-element.13.own_ref), channel_id=1, source_target_pairs={{0,1},{1,0},{2,3},{3,2},{4,5},{5,4},{6,7},{7,6},{8,9},{9,8},{10,11... | collective-permute-start | bytes 393224 | tf_op jit(solution)/shard_map/ppermute | solution.py:234

commit v5 on v4

--- a/solution.py
+++ b/solution.py
@@ -8,7 +8,6 @@
 from jax.sharding import PartitionSpec as P
 
 epsilon = 1e-05
-PANELS = tuple((max(f - 4, 0), f, f + 4) for f in range(0, 64, 4))
 shrink_weight = 0.5
 
 VMEM = pltpu.VMEM
@@ -81,8 +80,8 @@
     mean = jnp.sum(values, axis=0, keepdims=True) * (1.0 / samples)
     centered = values - mean
     var = jnp.sum(centered * centered, axis=0, keepdims=True) * (1.0 / samples)
-    scale = lax.rsqrt(var + epsilon)
-    standard = jnp.where(live > 0.0, centered * scale, 0.0).astype(bf16)
+    scale = lax.rsqrt(var + epsilon) * live
+    standard = (centered * scale).astype(bf16)
     standard_ref[...] = standard
     left = jnp.concatenate([high, mid, low, standard], axis=0)
     right = jnp.concatenate([standard, high, mid], axis=0)
@@ -98,8 +97,13 @@
     part_ref[rank + samples :, : 2 * rank] = jnp.concatenate([even, odd], axis=1)
 
 
-def factor_and_inverse(gram, panels):
+def factor_and_inverse(gram):
     rank = gram.shape[0]
+    group = 2
+    panels = [
+        (max(first - (4 if first < rank // 2 else 6), 0), first, first + group)
+        for first in range(0, rank, group)
+    ]
     row_ids = lax.broadcasted_iota(jnp.int32, (rank, rank), 0)
     col_ids = lax.broadcasted_iota(jnp.int32, (rank, rank), 1)
     eye = jnp.where(row_ids == col_ids, 1.0, 0.0).astype(f32)
@@ -113,22 +117,31 @@
     def row(tile, r):
         return jnp.broadcast_to(tile[r : r + 1, :], (8, lanes))
 
+    diagonal = None
     for k in range(rank):
         for start, first, last in panels:
             if start == k:
                 for j in range(first, last):
                     for t in range(j // 8, tiles):
-                        cols[j, t] = jnp.take_along_axis(work[t], jnp.full((8, lanes), j, jnp.int32), axis=1)
+                        cols[j, t] = jnp.take_along_axis(
+                            work[t], jnp.full((8, lanes), j, jnp.int32), axis=1
+                        )
         t0, r = k // 8, k % 8
-        root = lax.rsqrt(row(cols[k, t0], r))
+        if k == 0:
+            diagonal = row(cols[0, 0], 0)
+        root = lax.rsqrt(diagonal)
         square = root * root
+        if k + 1 < rank:
+            t1, r1 = (k + 1) // 8, (k + 1) % 8
+            side = row(cols[k, t1], r1)
+            diagonal = row(cols[k + 1, t1], r1) - side * side * square
         mult = {t: cols[k, t] * square for t in range(t0, tiles)}
-        mult[t0] = jnp.where(sublane > r, mult[t0], 0.0)
         for j in range(k + 1, rank):
             if (j, tiles - 1) in cols:
                 pivot = row(cols[k, j // 8], j % 8)
                 for t in range(j // 8, tiles):
                     cols[j, t] = cols[j, t] - mult[t] * pivot
+        mult[t0] = jnp.where(sublane > r, mult[t0], 0.0)
         pivot = row(work[t0], r)
         for t in range(t0, tiles):
             work[t] = work[t] - mult[t] * pivot
@@ -169,22 +182,28 @@
     mid = (image - high.astype(f32)).astype(bf16)
     for i, piece in enumerate((high, high, high, mid)):
         stack[i * rank : (i + 1) * rank, :] = piece
-    lower, inverse = factor_and_inverse(gram, PANELS)
+    lower, inverse = factor_and_inverse(gram)
     high = inverse.astype(bf16)
     mid = (inverse - high.astype(f32)).astype(bf16)
     left = jnp.concatenate(
         [jnp.concatenate([high, high], axis=1), jnp.concatenate([mid, mid], axis=1)], axis=0
     )
-    wide = dot(left, stack[...], NN)
-    new_buf[...] = wide[:rank] + wide[rank:]
-    new_copy = pltpu.make_async_copy(new_buf, new_ref, sems.at[1])
-    new_copy.start()
+    new_copies = []
+    parts = 2
+    width = new_buf.shape[1] // parts
+    for i in range(parts):
+        at = pl.ds(i * width, width)
+        wide = dot(left, stack[:, i * width : (i + 1) * width], NN)
+        new_buf[:, i * width : (i + 1) * width] = wide[:rank] + wide[rank:]
+        new_copies.append(pltpu.make_async_copy(new_buf.at[:, at], new_ref.at[:, at], sems.at[2 + i]))
+        new_copies[i].start()
     factor_buf[...] = lower
-    factor_copy = pltpu.make_async_copy(factor_buf, factor_ref, sems.at[2])
+    factor_copy = pltpu.make_async_copy(factor_buf, factor_ref, sems.at[1])
     factor_copy.start()
     image_copy.wait()
     factor_copy.wait()
-    new_copy.wait()
+    for copy in new_copies:
+        copy.wait()
 
 
 def body(genotypes, assignment, snp_counts, basis):
@@ -246,7 +265,7 @@
             pltpu.VMEM((rank, half), f32),
             pltpu.VMEM((rank, rank), f32),
             pltpu.VMEM((4 * rank, half), bf16),
-            pltpu.SemaphoreType.DMA((3,)),
+            pltpu.SemaphoreType.DMA((4,)),
         ],
         compiler_params=params,
         name="finish",

time: 24.8 us -> 24.6 us (level)
  no operation moved by 1% of the time
where the time goes in v5:
time: 24.6 us; the launch traced here: 24.4 us
  blocking collectives  18.1 us (74%)
  Pallas kernels  4.2 us (17%)
  waiting for transfers between devices  1.33 us (5%)
  between operations  0.66 us (3%)
    all_to_all x1, blocking collectives, body(): lax.all_to_all(ordered.reshape(blocks, samples, half), 'blk', split_axis=...  18.1 us
    pallas_call x1, Pallas kernels, body(): pl.pallas_call(functools.partial(finish_kernel, shrink_weight / total), o...  2.47 us
    ppermute x1, waiting for transfers between devices, body(): peer_part = lax.ppermute(part, 'row', [(0, 1), (1, 0)])  1.33 us
    pallas_call x1, Pallas kernels, body(): pl.pallas_call(functools.partial(order_kernel, samples, blocks, group, ha...  1.19 us
    pallas_call x1, Pallas kernels, body(): pl.pallas_call(project_kernel, out_shape=[jax.ShapeDtypeStruct((total, ha...  0.53 us
  transfers between devices with their start and end apart: 1, of which 1 were waited for; matrix products, arithmetic and copies ran while one was open for 0% of the time, Pallas kernels for 0%

profile of v5, /device:TPU:0, one launch (start us, length us, event | category | flops | bytes accessed | tf_op | source)
XLA Modules:
  0.0 24.4 jit_solution(14289217423156168660)
XLA Ops:
  0.6 1.2 %order.1 = (bf16[128,1024]{1,0:T(8,128)(2,1)S(1)}, f32[8,1024]{1,0:T(8,128)S(1)}) custom-call(s32[16]{0:T(128)} %assignment_ref.1, s32[16]{0:T(128)} %counts_ref.1, bf16[128,1024]{1,0:T(8,128)(2,1)} %bitcast.10), custom_call_target="tpu_custom_call" | custom-call | tf_op jit(solution)/shard_map/order/pallas_call | solution.py:217
  1.8 0.0 copy-start
  1.8 18.1 %all_to_all.5 = bf16[16,8,1024]{2,1,0:T(8,128)(2,1)S(1)} all-to-all(bf16[16,8,1024]{2,1,0:T(8,128)(2,1)S(1)} %bitcast.9), channel_id=1, replica_groups=mesh['blk'=16,'row'=2] {'blk'}, dimensions={0} | all-to-all | bytes 524288 | tf_op jit(solution)/shard_map/all_to_all | solution.py:237
  20.0 0.0 copy-done
  20.0 0.5 %project.1 = (bf16[128,1024]{1,0:T(8,128)(2,1)S(1)}, f32[64,1024]{1,0:T(8,128)S(1)}, f32[256,128]{1,0:T(8,128)S(1)}) custom-call(bf16[128,1024]{1,0:T(8,128)(2,1)S(1)} %bitcast.7, f32[8,1024]{1,0:T(8,128)S(1)} %get-tuple-element.12.live_ref, f32[64,1024]{1,0:T(8,128)S(1)} %bitcast.8), custom_call_target="tpu_custom_call" | custom-call | tf_op jit(solution)/shard_map/project/pallas_call | solution.py:241
  20.5 0.1 collective-permute-start
  20.6 1.3 %collective-permute-done.peer_ref = f32[256,128]{1,0:T(8,128)S(1)} collective-permute-done((f32[256,128]{1,0:T(8,128)S(1)}, f32[256,128]{1,0:T(8,128)S(1)}, u32[]{:S(2)}, u32[]{:S(2)}) %collective-permute-start) | collective-permute-done | bytes 131104 | tf_op jit(solution)/shard_map/ppermute | solution.py:253
  21.9 2.5 %finish.1 = (f32[64,1024]{1,0:T(8,128)}, f32[64,1024]{1,0:T(8,128)}, f32[64,64]{1,0:T(8,128)}) custom-call(f32[256,128]{1,0:T(8,128)S(1)} %get-tuple-element.13.own_ref, f32[256,128]{1,0:T(8,128)S(1)} %collective-permute-done.peer_ref, bf16[128,1024]{1,0:T(8,128)(2,1)S(1)} %get-tuple-element.14.standard_ref, f32[64,1024]{1,0:T(8,128)S(1)} %get-tuple-element.15.masked_ref), custom_call_target="tpu_custom_call" | custom-call | tf_op jit(solution)/shard_map/finish/pallas_call | solution.py:254
Async XLA Ops:
  1.8 18.2 %copy-start = (f32[1,64,1024]{2,1,0:T(8,128)S(1)}, f32[1,64,1024]{2,1,0:T(8,128)}, u32[]{:S(2)}) copy-start(f32[1,64,1024]{2,1,0:T(8,128)} %param.7) | copy-start | bytes 786436
  20.5 1.4 %collective-permute-start = (f32[256,128]{1,0:T(8,128)S(1)}, f32[256,128]{1,0:T(8,128)S(1)}, u32[]{:S(2)}, u32[]{:S(2)}) collective-permute-start(f32[256,128]{1,0:T(8,128)S(1)} %get-tuple-element.13.own_ref), channel_id=1, source_target_pairs={{0,1},{1,0},{2,3},{3,2},{4,5},{5,4},{6,7},{7,6},{8,9},{9,8},{10,11... | collective-permute-start | bytes 393224 | tf_op jit(solution)/shard_map/ppermute | solution.py:253

commit v6 on v5

--- a/solution.py
+++ b/solution.py
@@ -183,6 +183,9 @@
     for i, piece in enumerate((high, high, high, mid)):
         stack[i * rank : (i + 1) * rank, :] = piece
     lower, inverse = factor_and_inverse(gram)
+    factor_buf[...] = lower
+    factor_copy = pltpu.make_async_copy(factor_buf, factor_ref, sems.at[1])
+    factor_copy.start()
     high = inverse.astype(bf16)
     mid = (inverse - high.astype(f32)).astype(bf16)
     left = jnp.concatenate(
@@ -197,9 +200,6 @@
         new_buf[:, i * width : (i + 1) * width] = wide[:rank] + wide[rank:]
         new_copies.append(pltpu.make_async_copy(new_buf.at[:, at], new_ref.at[:, at], sems.at[2 + i]))
         new_copies[i].start()
-    factor_buf[...] = lower
-    factor_copy = pltpu.make_async_copy(factor_buf, factor_ref, sems.at[1])
-    factor_copy.start()
     image_copy.wait()
     factor_copy.wait()
     for copy in new_copies:

time: 24.6 us -> 24.6 us (level)
  no operation moved by 1% of the time
where the time goes in v6:
time: 24.6 us; the launch traced here: 24.4 us
  blocking collectives  18.1 us (74%)
  Pallas kernels  4.19 us (17%)
  waiting for transfers between devices  1.33 us (5%)
  between operations  0.66 us (3%)
    all_to_all x1, blocking collectives, body(): lax.all_to_all(ordered.reshape(blocks, samples, half), 'blk', split_axis=...  18.1 us
    pallas_call x1, Pallas kernels, body(): pl.pallas_call(functools.partial(finish_kernel, shrink_weight / total), o...  2.47 us
    ppermute x1, waiting for transfers between devices, body(): peer_part = lax.ppermute(part, 'row', [(0, 1), (1, 0)])  1.33 us
    pallas_call x1, Pallas kernels, body(): pl.pallas_call(functools.partial(order_kernel, samples, blocks, group, ha...  1.19 us
    pallas_call x1, Pallas kernels, body(): pl.pallas_call(project_kernel, out_shape=[jax.ShapeDtypeStruct((total, ha...  0.53 us
  transfers between devices with their start and end apart: 1, of which 1 were waited for; matrix products, arithmetic and copies ran while one was open for 0% of the time, Pallas kernels for 0%

profile of v6, /device:TPU:0, one launch (start us, length us, event | category | flops | bytes accessed | tf_op | source)
XLA Modules:
  0.0 24.4 jit_solution(818240260439444314)
XLA Ops:
  0.6 1.2 %order.1 = (bf16[128,1024]{1,0:T(8,128)(2,1)S(1)}, f32[8,1024]{1,0:T(8,128)S(1)}) custom-call(s32[16]{0:T(128)} %assignment_ref.1, s32[16]{0:T(128)} %counts_ref.1, bf16[128,1024]{1,0:T(8,128)(2,1)} %bitcast.10), custom_call_target="tpu_custom_call" | custom-call | tf_op jit(solution)/shard_map/order/pallas_call | solution.py:217
  1.8 0.0 copy-start
  1.8 18.1 %all_to_all.5 = bf16[16,8,1024]{2,1,0:T(8,128)(2,1)S(1)} all-to-all(bf16[16,8,1024]{2,1,0:T(8,128)(2,1)S(1)} %bitcast.9), channel_id=1, replica_groups=mesh['blk'=16,'row'=2] {'blk'}, dimensions={0} | all-to-all | bytes 524288 | tf_op jit(solution)/shard_map/all_to_all | solution.py:237
  20.0 0.0 copy-done
  20.0 0.5 %project.1 = (bf16[128,1024]{1,0:T(8,128)(2,1)S(1)}, f32[64,1024]{1,0:T(8,128)S(1)}, f32[256,128]{1,0:T(8,128)S(1)}) custom-call(bf16[128,1024]{1,0:T(8,128)(2,1)S(1)} %bitcast.7, f32[8,1024]{1,0:T(8,128)S(1)} %get-tuple-element.12.live_ref, f32[64,1024]{1,0:T(8,128)S(1)} %bitcast.8), custom_call_target="tpu_custom_call" | custom-call | tf_op jit(solution)/shard_map/project/pallas_call | solution.py:241
  20.5 0.1 collective-permute-start
  20.6 1.3 %collective-permute-done.peer_ref = f32[256,128]{1,0:T(8,128)S(1)} collective-permute-done((f32[256,128]{1,0:T(8,128)S(1)}, f32[256,128]{1,0:T(8,128)S(1)}, u32[]{:S(2)}, u32[]{:S(2)}) %collective-permute-start) | collective-permute-done | bytes 131104 | tf_op jit(solution)/shard_map/ppermute | solution.py:253
  21.9 2.5 %finish.1 = (f32[64,1024]{1,0:T(8,128)}, f32[64,1024]{1,0:T(8,128)}, f32[64,64]{1,0:T(8,128)}) custom-call(f32[256,128]{1,0:T(8,128)S(1)} %get-tuple-element.13.own_ref, f32[256,128]{1,0:T(8,128)S(1)} %collective-permute-done.peer_ref, bf16[128,1024]{1,0:T(8,128)(2,1)S(1)} %get-tuple-element.14.standard_ref, f32[64,1024]{1,0:T(8,128)S(1)} %get-tuple-element.15.masked_ref), custom_call_target="tpu_custom_call" | custom-call | tf_op jit(solution)/shard_map/finish/pallas_call | solution.py:254
Async XLA Ops:
  1.8 18.2 %copy-start = (f32[1,64,1024]{2,1,0:T(8,128)S(1)}, f32[1,64,1024]{2,1,0:T(8,128)}, u32[]{:S(2)}) copy-start(f32[1,64,1024]{2,1,0:T(8,128)} %param.7) | copy-start | bytes 786436
  20.5 1.4 %collective-permute-start = (f32[256,128]{1,0:T(8,128)S(1)}, f32[256,128]{1,0:T(8,128)S(1)}, u32[]{:S(2)}, u32[]{:S(2)}) collective-permute-start(f32[256,128]{1,0:T(8,128)S(1)} %get-tuple-element.13.own_ref), channel_id=1, source_target_pairs={{0,1},{1,0},{2,3},{3,2},{4,5},{5,4},{6,7},{7,6},{8,9},{9,8},{10,11... | collective-permute-start | bytes 393224 | tf_op jit(solution)/shard_map/ppermute | solution.py:253

commit v7 on v6

--- a/solution.py
+++ b/solution.py
@@ -99,9 +99,9 @@
 
 def factor_and_inverse(gram):
     rank = gram.shape[0]
-    group = 2
+    group = 4
     panels = [
-        (max(first - (4 if first < rank // 2 else 6), 0), first, first + group)
+        (max(first - (4 if first < rank // 2 else 8), 0), first, first + group)
         for first in range(0, rank, group)
     ]
     row_ids = lax.broadcasted_iota(jnp.int32, (rank, rank), 0)

time: 24.6 us -> 24.6 us (level)
  no operation moved by 1% of the time
where the time goes in v7:
time: 24.6 us; the launch traced here: 24.4 us
  blocking collectives  18.1 us (74%)
  Pallas kernels  4.2 us (17%)
  waiting for transfers between devices  1.33 us (5%)
  between operations  0.66 us (3%)
    all_to_all x1, blocking collectives, body(): lax.all_to_all(ordered.reshape(blocks, samples, half), 'blk', split_axis=...  18.1 us
    pallas_call x1, Pallas kernels, body(): pl.pallas_call(functools.partial(finish_kernel, shrink_weight / total), o...  2.47 us
    ppermute x1, waiting for transfers between devices, body(): peer_part = lax.ppermute(part, 'row', [(0, 1), (1, 0)])  1.33 us
    pallas_call x1, Pallas kernels, body(): pl.pallas_call(functools.partial(order_kernel, samples, blocks, group, ha...  1.19 us
    pallas_call x1, Pallas kernels, body(): pl.pallas_call(project_kernel, out_shape=[jax.ShapeDtypeStruct((total, ha...  0.53 us
  transfers between devices with their start and end apart: 1, of which 1 were waited for; matrix products, arithmetic and copies ran while one was open for 0% of the time, Pallas kernels for 0%

profile of v7, /device:TPU:0, one launch (start us, length us, event | category | flops | bytes accessed | tf_op | source)
XLA Modules:
  0.0 24.4 jit_solution(8068673462267857971)
XLA Ops:
  0.6 1.2 %order.1 = (bf16[128,1024]{1,0:T(8,128)(2,1)S(1)}, f32[8,1024]{1,0:T(8,128)S(1)}) custom-call(s32[16]{0:T(128)} %assignment_ref.1, s32[16]{0:T(128)} %counts_ref.1, bf16[128,1024]{1,0:T(8,128)(2,1)} %bitcast.10), custom_call_target="tpu_custom_call" | custom-call | tf_op jit(solution)/shard_map/order/pallas_call | solution.py:217
  1.8 0.0 copy-start
  1.8 18.1 %all_to_all.5 = bf16[16,8,1024]{2,1,0:T(8,128)(2,1)S(1)} all-to-all(bf16[16,8,1024]{2,1,0:T(8,128)(2,1)S(1)} %bitcast.9), channel_id=1, replica_groups=mesh['blk'=16,'row'=2] {'blk'}, dimensions={0} | all-to-all | bytes 524288 | tf_op jit(solution)/shard_map/all_to_all | solution.py:237
  20.0 0.0 copy-done
  20.0 0.5 %project.1 = (bf16[128,1024]{1,0:T(8,128)(2,1)S(1)}, f32[64,1024]{1,0:T(8,128)S(1)}, f32[256,128]{1,0:T(8,128)S(1)}) custom-call(bf16[128,1024]{1,0:T(8,128)(2,1)S(1)} %bitcast.7, f32[8,1024]{1,0:T(8,128)S(1)} %get-tuple-element.12.live_ref, f32[64,1024]{1,0:T(8,128)S(1)} %bitcast.8), custom_call_target="tpu_custom_call" | custom-call | tf_op jit(solution)/shard_map/project/pallas_call | solution.py:241
  20.5 0.1 collective-permute-start
  20.6 1.3 %collective-permute-done.peer_ref = f32[256,128]{1,0:T(8,128)S(1)} collective-permute-done((f32[256,128]{1,0:T(8,128)S(1)}, f32[256,128]{1,0:T(8,128)S(1)}, u32[]{:S(2)}, u32[]{:S(2)}) %collective-permute-start) | collective-permute-done | bytes 131104 | tf_op jit(solution)/shard_map/ppermute | solution.py:253
  21.9 2.5 %finish.1 = (f32[64,1024]{1,0:T(8,128)}, f32[64,1024]{1,0:T(8,128)}, f32[64,64]{1,0:T(8,128)}) custom-call(f32[256,128]{1,0:T(8,128)S(1)} %get-tuple-element.13.own_ref, f32[256,128]{1,0:T(8,128)S(1)} %collective-permute-done.peer_ref, bf16[128,1024]{1,0:T(8,128)(2,1)S(1)} %get-tuple-element.14.standard_ref, f32[64,1024]{1,0:T(8,128)S(1)} %get-tuple-element.15.masked_ref), custom_call_target="tpu_custom_call" | custom-call | tf_op jit(solution)/shard_map/finish/pallas_call | solution.py:254
Async XLA Ops:
  1.8 18.2 %copy-start = (f32[1,64,1024]{2,1,0:T(8,128)S(1)}, f32[1,64,1024]{2,1,0:T(8,128)}, u32[]{:S(2)}) copy-start(f32[1,64,1024]{2,1,0:T(8,128)} %param.7) | copy-start | bytes 786436
  20.5 1.4 %collective-permute-start = (f32[256,128]{1,0:T(8,128)S(1)}, f32[256,128]{1,0:T(8,128)S(1)}, u32[]{:S(2)}, u32[]{:S(2)}) collective-permute-start(f32[256,128]{1,0:T(8,128)S(1)} %get-tuple-element.13.own_ref), channel_id=1, source_target_pairs={{0,1},{1,0},{2,3},{3,2},{4,5},{5,4},{6,7},{7,6},{8,9},{9,8},{10,11... | collective-permute-start | bytes 393224 | tf_op jit(solution)/shard_map/ppermute | solution.py:253
